TPU v7x, 32 devices: a whole 2x2x4 slice. The times are simulated.
32 devices in a mesh: row: 4 (over z), col: 4 (over y, x), layer: 2 (over core).
Axes of the slice: x: 2, y: 2, z: 4, core: 2. Of those that a mesh axis runs over, the one named last changes fastest.
Arguments:
- expression: bfloat16 [6144, 1024], P(('row', 'col'), 'layer'), may hold values from -240 to 240
Outputs:
- connectivity: float32 [6144], P(('row', 'col', 'layer'))
All inputs are finite; a program needn't handle non-finite values.
Results may differ from a plain program's by a relative error of at most 0.00048.
Values may be sent and summed in bfloat16 or wider, within the bound.
A program may use at most 64 MiB of HBM per device.

v0:
```python
import functools

import jax
import jax.numpy as jnp
from jax import lax
from jax.experimental import pallas as pl
from jax.experimental.pallas import tpu as pltpu
from jax.sharding import PartitionSpec as P

MESH = pl.DeviceIdType.MESH
epsilon = 1e-05


def flip(c, k):
    bit = 1
    while bit <= k:
        if k & bit:
            c = c + bit - 2 * bit * lax.rem(lax.div(c, bit), 2)
        bit *= 2
    return c


def kernel(rows, cols, x_ref, out_ref, raw, own, panel, far_raw, far, pacc, racc, psrc, pdst, rsrc, rdst,
           in_sem, ex_sem, ps_sem, pr_sem, zs_sem, zr_sem, xs_sem, xr_sem, qs_sem, qr_sem, ts_sem, tr_sem):
    p, c, l = lax.axis_index("row"), lax.axis_index("col"), lax.axis_index("layer")
    genes, part = x_ref.shape
    half = genes // 2
    samples = 2 * part
    depth, pieces, piece = far.shape[0], far.shape[1], far.shape[2]
    other = 1 - l
    order = [k for k in range(cols) if k != 3] + [3]
    last = cols - 1

    def rows_of(first, stop):
        return pl.ds(first * half, (stop - first) * half)

    def remote(src, dst, send, recv, device):
        return pltpu.make_async_remote_copy(
            src_ref=src, dst_ref=dst, send_sem=send, recv_sem=recv, device_id=device, device_id_type=MESH
        )

    load = pltpu.make_async_copy(x_ref, raw.at[l], in_sem)
    load.start()

    barrier = pltpu.get_barrier_semaphore()
    greeted = [(lax.rem(p + r, rows), c, h) for r in range(1, rows) for h in range(2)]
    greeted += [(p, flip(c, k), l) for k in range(1, cols)] + [(p, c, other)]
    for device in greeted:
        pl.semaphore_signal(barrier, inc=1, device_id=device, device_id_type=MESH)
    pacc[...] = jnp.zeros_like(pacc)
    racc[...] = jnp.zeros_like(racc)
    load.wait()
    pl.semaphore_wait(barrier, len(greeted))

    odd = lax.rem(lax.rem(p, depth), 2) == 1
    is_low = p < depth
    sends_last = odd == is_low
    receives_last = odd != is_low

    def far_copy(d, i):
        at = pl.ds(pl.multiple_of(i * piece, piece), piece)
        return remote(raw.at[l, at], far_raw.at[d, i, l], zs_sem.at[d, i], zr_sem.at[d, i],
                      (lax.rem(p + d + 1, rows), c, l))

    def relay(d, i):
        return remote(far_raw.at[d, i, l], far_raw.at[d, i, l], xs_sem.at[d, i], xr_sem.at[d, i], (p, c, other))

    for d in range(depth - 1):
        for i in range(pieces):
            far_copy(d, i).start()

    @pl.when(sends_last)
    def _():
        for i in range(pieces):
            far_copy(depth - 1, i).start()

    exchange = remote(raw.at[l], raw.at[l], ex_sem.at[0], ex_sem.at[1], (p, c, other))
    exchange.start()
    exchange.wait_recv()

    step = 32

    def scale(low, high):
        low, high = low.astype(jnp.float32), high.astype(jnp.float32)
        total = jnp.sum(low, axis=1, keepdims=True) + jnp.sum(high, axis=1, keepdims=True)
        squares = jnp.sum(low * low + high * high, axis=1, keepdims=True)
        average = total / samples
        variance = squares / samples - average * average
        gain = lax.rsqrt(variance + epsilon)
        return (((low - average) * gain).astype(jnp.bfloat16), ((high - average) * gain).astype(jnp.bfloat16))

    def standardize(h):
        for i in range(half // step):
            at = pl.ds(pl.multiple_of(h * half + i * step, step), step)
            low, high = scale(raw[0, at, :], raw[1, at, :])
            own[at, 0:part] = low
            own[at, part:samples] = high

    def standardize_far(d, i):
        for j in range(piece // step):
            at = pl.ds(j * step, step)
            low, high = scale(far_raw[d, i, 0, at, :], far_raw[d, i, 1, at, :])
            far[d, i, at, 0:part] = low
            far[d, i, at, part:samples] = high

    standardize(l)
    mine_at = pl.ds(pl.multiple_of(l * half, half), half)
    cut = half // 2

    def panel_copy(k, s):
        at = pl.ds(pl.multiple_of(l * half + s * cut, cut), cut)
        return remote(own.at[at], panel.at[pl.ds(order.index(k) * half + s * cut, cut)], ps_sem.at[k - 1, s], pr_sem.at[k - 1, s],
                      (p, flip(c, k), l))

    def pass_on(s):
        source, target = (2, 1) if s == 0 else (1, 2)
        return remote(panel.at[pl.ds(source * half + s * cut, cut)], panel.at[pl.ds(last * half + s * cut, cut)],
                      ps_sem.at[2, s], pr_sem.at[2, s], (p, flip(c, target), l))

    direct = [k for k in range(1, cols) if k != 3]
    panel_copies = {(k, s): panel_copy(k, s) for k in direct for s in range(2)}
    panel_copies.update({(3, s): pass_on(s) for s in range(2)})
    for k, s in [(1, 1), (2, 0), (1, 0), (2, 1)] + [(k, s) for k in direct[2:] for s in range(2)]:
        panel_copies[k, s].start()

    standardize(other)
    panel[rows_of(0, 1), :] = own[mine_at, :]

    def adjacency(at, block):
        product = lax.dot_general(
            panel[at, :], block, (((1,), (1,)), ((), ())), preferred_element_type=jnp.float32
        )
        shifted = product * (0.5 / samples) + 0.5
        square = shifted * shifted
        fourth = square * square
        eighth = fourth * fourth
        return eighth * fourth

    def own_pairs(first, stop):
        at = rows_of(first, stop)
        value = adjacency(at, own[...])
        lanes = value[:, 0:128]
        for j in range(1, genes // 128):
            lanes = lanes + value[:, j * 128:(j + 1) * 128]
        pacc[at, :] += lanes

    def far_pairs(first, stop, e):
        d, i = event(e)
        at = rows_of(first, stop)
        value = adjacency(at, far[d, i])
        pacc[at, :] += value
        racc[d, i] += jnp.sum(value.reshape(value.shape[0] // 8, 8, piece), axis=0)

    count = pieces * jnp.where(receives_last, depth, depth - 1)

    def event(e):
        return lax.div(e, pieces), lax.rem(e, pieces)

    own_pairs(0, 1)
    for s in range(2):
        panel_copies[2 - s, s].wait_recv()
        panel_copies[3, s].start()

    def take(e):
        d, i = event(e)
        far_copy(d, i).wait_recv()
        relay(d, i).start()

    def ready(e):
        d, i = event(e)
        relay(d, i).wait_recv()
        standardize_far(d, i)

    take(0)
    ready(0)
    take(1)
    take(2)
    ready(1)
    for s in range(2):
        panel_copies[1 + s, s].wait_recv()
    for k in direct[2:]:
        for s in range(2):
            panel_copies[k, s].wait_recv()
    own_pairs(1, last)
    longer = count > 3

    @pl.when(longer)
    def _():
        take(3)

    @pl.loop(0, count - 2)
    def _(e):
        @pl.when(e > 1)
        def _():
            @pl.when(e > 3)
            def _():
                take(e)

            ready(e)

        far_pairs(0, last, e)

    for s in range(2):
        panel_copies[3, s].wait_recv()
    own_pairs(last, cols)

    @pl.loop(0, count - 2)
    def _(e):
        far_pairs(last, cols, e)

    @pl.when(longer)
    def _():
        take(count - 2)
        take(count - 1)
        ready(count - 2)

    far_pairs(0, last, count - 2)
    far_pairs(last, cols, count - 2)
    ready(count - 1)
    far_pairs(0, last, count - 1)
    far_pairs(last, cols, count - 1)

    def fold(k):
        at = order.index(k)
        turned = pacc[rows_of(at, at + 1), :].T
        return jnp.sum(turned.reshape(128 // 8, 8, half), axis=0)

    def give_back(d):
        total = jnp.concatenate([racc[d, i] for i in range(pieces)], axis=1)
        home = lax.rem(p + rows - d - 1, rows)
        for h in range(2):
            rsrc[d, h] = total[:, h * half:(h + 1) * half]
            remote(rsrc.at[d, h], rdst.at[d, l], ts_sem.at[d, h], tr_sem.at[d, l], (home, c, h)).start()

    for d in range(depth - 1):
        give_back(d)

    @pl.when(receives_last)
    def _():
        give_back(depth - 1)

    part_copies = []
    for k in range(cols - 1, 0, -1):
        psrc[k - 1] = fold(k)
        copy = remote(psrc.at[k - 1], pdst.at[k - 1], qs_sem.at[k - 1], qr_sem.at[k - 1], (p, flip(c, k), l))
        copy.start()
        part_copies.append(copy)
    total = fold(0) - 1.0 / 8
    for copy in part_copies:
        copy.wait_recv()
    for k in range(1, cols):
        total = total + pdst[k - 1]

    def back_copy(d, h):
        return remote(rsrc.at[d, h], rdst.at[d, h], ts_sem.at[d, h], tr_sem.at[d, h], (p, c, other))

    for d in range(depth - 1):
        for h in range(2):
            back_copy(d, h).wait_recv()
            total = total + rdst[d, h]

    out_ref[...] = jnp.sum(total, axis=0)

    @pl.when(sends_last)
    def _():
        extra = jnp.zeros_like(total)
        for h in range(2):
            back_copy(depth - 1, h).wait_recv()
            extra = extra + rdst[depth - 1, h]
        out_ref[...] += jnp.sum(extra, axis=0)
        for i in range(pieces):
            far_copy(depth - 1, i).wait_send()

    exchange.wait_send()
    for copy in list(panel_copies.values()) + part_copies:
        copy.wait_send()
    for d in range(depth - 1):
        for i in range(pieces):
            far_copy(d, i).wait_send()
            relay(d, i).wait_send()
        for h in range(2):
            back_copy(d, h).wait_send()

    @pl.when(receives_last)
    def _():
        for i in range(pieces):
            relay(depth - 1, i).wait_send()
        for h in range(2):
            back_copy(depth - 1, h).wait_send()


def solution(mesh):
    rows, cols = mesh.shape["row"], mesh.shape["col"]
    depth = rows // 2
    piece = 128
    dma = lambda *shape: pltpu.SemaphoreType.DMA(shape)

    def on_device(expression):
        genes, part = expression.shape
        half, samples, pieces = genes // 2, 2 * part, genes // piece
        summed = pl.pallas_call(
            functools.partial(kernel, rows, cols),
            out_shape=jax.ShapeDtypeStruct((half,), jnp.float32),
            in_specs=[pl.BlockSpec(memory_space=pl.ANY)],
            out_specs=pl.BlockSpec(memory_space=pltpu.VMEM),
            scratch_shapes=[
                pltpu.VMEM((2, genes, part), jnp.bfloat16),
                pltpu.VMEM((genes, samples), jnp.bfloat16),
                pltpu.VMEM((cols * half, samples), jnp.bfloat16),
                pltpu.VMEM((depth, pieces, 2, piece, part), jnp.bfloat16),
                pltpu.VMEM((depth, pieces, piece, samples), jnp.bfloat16),
                pltpu.VMEM((cols * half, 128), jnp.float32),
                pltpu.VMEM((depth, pieces, 8, piece), jnp.float32),
                pltpu.VMEM((cols - 1, 8, half), jnp.float32),
                pltpu.VMEM((cols - 1, 8, half), jnp.float32),
                pltpu.VMEM((depth, 2, 8, half), jnp.float32),
                pltpu.VMEM((depth, 2, 8, half), jnp.float32),
                pltpu.SemaphoreType.DMA,
                dma(2),
                dma(cols - 1, 2), dma(cols - 1, 2),
                dma(depth, pieces), dma(depth, pieces),
                dma(depth, pieces), dma(depth, pieces),
                dma(cols - 1), dma(cols - 1),
                dma(depth, 2), dma(depth, 2),
            ],
            compiler_params=pltpu.CompilerParams(collective_id=0, has_side_effects=True),
        )(expression)
        return summed

    return jax.shard_map(
        on_device,
        mesh=mesh,
        in_specs=(P(("row", "col"), "layer"),),
        out_specs=P(("row", "col", "layer")),
        check_vma=False,
    )
```

profile of v0, /device:TPU:0, one launch (start us, length us, event | category | flops | bytes accessed | tf_op | source)
XLA Modules:
  0.0 32.1 jit_solution(6338765448054986819)
XLA Ops:
  0.0 30.9 %shard_map.17 = f32[192]{0:T(256)} custom-call(bf16[384,512]{1,0:T(8,128)(2,1)} %x_ref.1), custom_call_target="tpu_custom_call" | custom-call | tf_op jit(solution)/shard_map/pallas_call | solution.py:301
  30.9 1.2 %copy.3 = f32[192]{0:T(256)} copy(f32[192]{0:T(256)} %shard_map.17) | data formatting | bytes 1536
where the time goes:
time: 32.3 us; the launch traced here: 32.1 us
  Pallas kernels  30.9 us (96%)
  local copies, waits for them, and re-layouts  1.24 us (4%)
    pallas_call x1, Pallas kernels, on_device(): pl.pallas_call(functools.partial(kernel, rows, cols), out_shape=jax.Shape...  30.9 us
    unnamed x1, local copies, waits for them, and re-layouts  1.24 us

commit v1 on v0

--- a/solution.py
+++ b/solution.py
@@ -323,8 +323,8 @@
                 dma(cols - 1), dma(cols - 1),
                 dma(depth, 2), dma(depth, 2),
             ],
-            compiler_params=pltpu.CompilerParams(collective_id=0, has_side_effects=True),
-        )(expression)
+            compiler_params=pltpu.CompilerParams(collective_id=0, has_side_effects=True, vmem_limit_bytes=48000000),
+        )(pltpu.with_memory_space_constraint(expression, pltpu.HBM))
         return summed
 
     return jax.shard_map(

time: 32.3 us -> 31 us (0.960)
  local copies, waits for them, and re-layouts: 1.24 us -> 0.56 us
  Pallas kernels: 30.9 us -> 30.3 us
    unnamed x1, local copies, waits for them, and re-layouts: 1.24 us -> 0.56 us
    pallas_call x1, Pallas kernels: 30.9 us -> 30.3 us  [on_device(): pl.pallas_call(functools.partial(kernel, rows, cols), out_shape=jax.Shape...]
where the time goes in v1:
time: 31 us; the launch traced here: 30.9 us
  Pallas kernels  30.3 us (98%)
  local copies, waits for them, and re-layouts  0.56 us (2%)
    pallas_call x1, Pallas kernels, on_device(): pl.pallas_call(functools.partial(kernel, rows, cols), out_shape=jax.Shape...  30.3 us

profile of v1, /device:TPU:0, one launch (start us, length us, event | category | flops | bytes accessed | tf_op | source)
XLA Modules:
  0.0 30.9 jit_solution(8359503188688361218)
XLA Ops:
  0.0 30.3 %shard_map.17 = f32[192]{0:T(256)S(1)} custom-call(bf16[384,512]{1,0:T(8,128)(2,1)} %x_ref.1), custom_call_target="tpu_custom_call" | custom-call | tf_op jit(solution)/shard_map/pallas_call | solution.py:301
  30.3 0.6 %copy.3 = f32[192]{0:T(256)} copy(f32[192]{0:T(256)S(1)} %shard_map.17) | data formatting | bytes 1536

commit v2 on v1

v2 whole, which is shorter than its diff:
```python
import functools

import jax
import jax.numpy as jnp
from jax import lax
from jax.experimental import pallas as pl
from jax.experimental.pallas import tpu as pltpu
from jax.sharding import PartitionSpec as P

MESH = pl.DeviceIdType.MESH
epsilon = 1e-05


def flip(c, k):
    bit = 1
    while bit <= k:
        if k & bit:
            c = c + bit - 2 * bit * lax.rem(lax.div(c, bit), 2)
        bit *= 2
    return c


def is_above(c, k):
    top = 1 << (k.bit_length() - 1)
    return lax.rem(lax.div(c, top), 2) == 0


def plan(rows):
    if rows == 4:
        return [(1, 0, None), (3, 1, None), (3, 0, 1), (0, 2, None), (1, 2, None), (2, 3, None)]
    flows = []
    for d in range(1, rows // 2 + 1):
        for s in range(rows if 2 * d < rows else rows // 2):
            flows.append((s, (s + d) % rows, None))
    return flows


def kernel(rows, cols, x_ref, out_ref, praw, panel, far_raw, far, pacc, racc, psrc, pdst, rsrc, rdst,
           in_sem, ex_sem, ps_sem, pr_sem, fs_sem, fr_sem, zs_sem, zr_sem, xs_sem, qs_sem, qr_sem, ts_sem, tr_sem,
           x_ready, z_ready):
    p, c, l = lax.axis_index("row"), lax.axis_index("col"), lax.axis_index("layer")
    genes, part = x_ref.shape
    half = genes // 2
    piece = half // 2
    samples = 2 * part
    other = 1 - l
    order = [k for k in range(cols) if k != 3] + [3]
    direct = [k for k in range(1, cols) if k != 3]
    last = cols - 1
    flows = plan(rows)
    slots = {t: [f for f in flows if f[1] == t] for t in range(rows)}
    outs = {s: [f for f in flows if f[0] == s and f[2] is None] for s in range(rows)}
    back = {s: [f for f in flows if f[0] == s] for s in range(rows)}
    pairs_of = {q: sorted({f[1] for f in flows if f[0] == q} | {f[0] for f in flows if f[1] == q}) for q in range(rows)}

    def remote(src, dst, send, recv, device):
        return pltpu.make_async_remote_copy(
            src_ref=src, dst_ref=dst, send_sem=send, recv_sem=recv, device_id=device, device_id_type=MESH
        )

    def by_row(values):
        value = values[0]
        for q in range(1, rows):
            value = jnp.where(p == q, values[q], value)
        return value

    def at_row(q, condition=True):
        return pl.when(p == q)

    load = pltpu.make_async_copy(x_ref, praw.at[0, l], in_sem)
    load.start()

    barrier = pltpu.get_barrier_semaphore()

    def greet(device):
        pl.semaphore_signal(barrier, inc=1, device_id=device, device_id_type=MESH)

    greet((p, c, other))
    for k in direct:
        @pl.when(is_above(c, k))
        def _():
            greet((p, flip(c, k), l))
    for q in range(rows):
        above = [t for t in pairs_of[q] if t > q]
        if above:
            @pl.when(p == q)
            def _():
                for t in above:
                    for h in range(2):
                        greet((t, c, h))
    greetings = 1 + by_row([2 * len([t for t in pairs_of[q] if t < q]) for q in range(rows)])
    for k in direct:
        greetings = greetings + jnp.where(is_above(c, k), 0, 1)

    pacc[...] = jnp.zeros_like(pacc)
    racc[...] = jnp.zeros_like(racc)
    pl.semaphore_wait(barrier, greetings)
    for k in direct:
        @pl.when(jnp.logical_not(is_above(c, k)))
        def _():
            pl.semaphore_signal(x_ready.at[k - 1], inc=1, device_id=(p, flip(c, k), l), device_id_type=MESH)
    for t in range(rows):
        below = [f for f in slots[t] if f[2] is None and f[0] < t]
        if below:
            @pl.when(p == t)
            def _():
                for f in below:
                    for h in range(2):
                        pl.semaphore_signal(z_ready.at[outs[f[0]].index(f)], inc=1, device_id=(f[0], c, h), device_id_type=MESH)
    load.wait()

    def z_copy(f, h, i):
        source = praw.at[0, l, pl.ds(h * half + i * piece, piece)]
        return remote(source, far_raw.at[slots[f[1]].index(f), l, pl.ds(i * piece, piece)],
                      zs_sem.at[outs[f[0]].index(f), h, i], zr_sem.at[slots[f[1]].index(f), l, i], (f[1], c, h))

    def z_arrival(t, b, i):
        at = far_raw.at[t, b, pl.ds(pl.multiple_of(i * piece, piece), piece)]
        return remote(at, at, zs_sem.at[0, 0, 0], zr_sem.at[t, b, i], (p, c, other))

    def held_back(f):
        return rows == 4 and f == (1, 2, None)

    def send_row(f):
        for i in range(1 if held_back(f) else 2):
            for h in range(2):
                z_copy(f, h, i).start()

    exchange = remote(praw.at[0, l], praw.at[0, l], ex_sem.at[0], ex_sem.at[1], (p, c, other))
    exchange.start()
    for q in range(rows):
        down = [f for f in outs[q] if f[1] < q]
        if down:
            @pl.when(p == q)
            def _():
                for f in down:
                    send_row(f)

    def panel_copy(k, s):
        at = pl.ds(s * half, half)
        return remote(praw.at[0, l, at], praw.at[order.index(k), l, at], ps_sem.at[k - 1, s], pr_sem.at[k - 1, s],
                      (p, flip(c, k), l))

    def pass_on(s):
        source, target = (2, 1) if s == 0 else (1, 2)
        at = pl.ds(s * half, half)
        return remote(praw.at[order.index(source), l, at], praw.at[last, l, at], ps_sem.at[2, s], pr_sem.at[2, s],
                      (p, flip(c, target), l))

    panel_copies = {(k, s): panel_copy(k, s) for k in direct for s in range(2)}
    panel_copies.update({(3, s): pass_on(s) for s in range(2)})

    def forward(k, s):
        at = praw.at[order.index(k), l, pl.ds(s * half, half)]
        return remote(at, at, fs_sem.at[k - 1, s], fr_sem.at[k - 1, s], (p, c, other))

    first = {1: (1, 0), 2: (0, 1)}
    for k in direct:
        @pl.when(jnp.logical_not(is_above(c, k)))
        def _():
            for s in first.get(k, (0, 1)):
                panel_copies[k, s].start()
    for k in direct:
        @pl.when(is_above(c, k))
        def _():
            pl.semaphore_wait(x_ready.at[k - 1], 1)
            for s in first.get(k, (0, 1)):
                panel_copies[k, s].start()
    for q in range(rows):
        up = [f for f in outs[q] if f[1] > q]
        if up:
            @pl.when(p == q)
            def _():
                for f in up:
                    pl.semaphore_wait(z_ready.at[outs[q].index(f)], 2)
                    send_row(f)

    step = 32

    def scale(low, high):
        low, high = low.astype(jnp.float32), high.astype(jnp.float32)
        total = jnp.sum(low, axis=1, keepdims=True) + jnp.sum(high, axis=1, keepdims=True)
        squares = jnp.sum(low * low + high * high, axis=1, keepdims=True)
        average = total / samples
        variance = squares / samples - average * average
        gain = lax.rsqrt(variance + epsilon)
        return (((low - average) * gain).astype(jnp.bfloat16), ((high - average) * gain).astype(jnp.bfloat16))

    def standardize(k):
        n = order.index(k)
        for i in range(genes // step):
            low, high = scale(praw[n, 0, pl.ds(i * step, step), :], praw[n, 1, pl.ds(i * step, step), :])
            at = pl.ds(n * genes + i * step, step)
            panel[at, 0:part] = low
            panel[at, part:samples] = high

    def standardize_far(t, i):
        for j in range(piece // step):
            at = pl.ds(pl.multiple_of(i * piece + j * step, step), step)
            low, high = scale(far_raw[t, 0, at, :], far_raw[t, 1, at, :])
            far[t, at, 0:part] = low
            far[t, at, part:samples] = high

    def adjacency(block, start, stop):
        product = lax.dot_general(
            block, panel[start * genes:stop * genes, :], (((1,), (1,)), ((), ())), preferred_element_type=jnp.float32
        )
        shifted = product * (0.5 / samples) + 0.5
        square = shifted * shifted
        fourth = square * square
        eighth = fourth * fourth
        return eighth * fourth

    def own_pairs(start, stop):
        at = pl.ds(pl.multiple_of(l * half, half), half)
        value = adjacency(panel[at, :], start, stop)
        pacc[:, start * genes:stop * genes] += jnp.sum(value.reshape(half // 8, 8, value.shape[1]), axis=0)

    def far_pairs(t, i, start, stop):
        at = pl.ds(pl.multiple_of(i * piece, piece), piece)
        value = adjacency(far[t, at, :], start, stop)
        pacc[:, start * genes:stop * genes] += jnp.sum(value.reshape(piece // 8, 8, value.shape[1]), axis=0)
        lanes = value[:, 0:128]
        for j in range(1, value.shape[1] // 128):
            lanes = lanes + value[:, j * 128:(j + 1) * 128]
        racc[t, at, :] += lanes

    exchange.wait_recv()
    standardize(0)
    own_pairs(0, 1)

    relays = [f for f in flows if f[2] is not None]

    def relay_copy(f, b, i):
        t = slots[f[2]].index((f[0], f[2], None))
        at = pl.ds(i * piece, piece)
        return remote(far_raw.at[t, b, at], far_raw.at[slots[f[1]].index(f), b, at],
                      xs_sem.at[b, i], zr_sem.at[slots[f[1]].index(f), b, i], (f[1], c, l))

    def relay(i):
        for f in relays:
            @pl.when(p == f[2])
            def _():
                for b in range(2):
                    z_arrival(slots[f[2]].index((f[0], f[2], None)), b, i).wait_recv()
                    relay_copy(f, b, i).start()

    for s in range(2):
        panel_copies[2 - s, s].wait_recv()
        panel_copies[3, s].start()
        forward(2 - s, s).start()
    relay(0)
    for s in range(2):
        panel_copies[1 + s, s].wait_recv()
        forward(1 + s, s).start()
    for k in direct[2:]:
        for s in range(2):
            panel_copies[k, s].wait_recv()
            forward(k, s).start()
    relay(1)
    for f in flows:
        if held_back(f):
            @pl.when(p == f[0])
            def _():
                for h in range(2):
                    z_copy(f, h, 1).start()
    for k in direct:
        for s in range(2):
            forward(k, s).wait_recv()
        standardize(k)
    own_pairs(1, last)

    def take_far(t, i):
        passing = [f[2] for f in relays if slots[f[2]].index((f[0], f[2], None)) == t]
        if passing:
            @pl.when(p != passing[0])
            def _():
                for b in range(2):
                    z_arrival(t, b, i).wait_recv()
        else:
            for b in range(2):
                z_arrival(t, b, i).wait_recv()
        standardize_far(t, i)

    def give_back(t):
        turned = racc[t].T
        rsrc[t] = jnp.sum(turned.reshape(128 // 8, 8, half), axis=0)
        for q in range(rows):
            if t < len(slots[q]):
                @pl.when(p == q)
                def _():
                    back_copy(slots[q][t]).start()

    def back_copy(f):
        t, j = slots[f[1]].index(f), back[f[0]].index(f)
        return remote(rsrc.at[t], rdst.at[j], ts_sem.at[t], tr_sem.at[j], (f[0], c, l))

    @pl.loop(0, 2)
    def _(i):
        take_far(0, i)
        far_pairs(0, i, 0, last)

    for s in range(2):
        panel_copies[3, s].wait_recv()
        forward(3, s).start()
    for s in range(2):
        forward(3, s).wait_recv()
    standardize(3)
    own_pairs(last, cols)

    @pl.loop(0, 2)
    def _(i):
        far_pairs(0, i, last, cols)

    give_back(0)
    depth = max(len(slots[q]) for q in range(rows))
    for t in range(1, depth):
        @pl.when(by_row([len(slots[q]) for q in range(rows)]) > t)
        def _():
            @pl.loop(0, 2)
            def _(i):
                take_far(t, i)
                far_pairs(t, i, 0, cols)

            give_back(t)

    def part_copy(k, h):
        return remote(psrc.at[k, h], pdst.at[k, l], qs_sem.at[k, h], qr_sem.at[k, l], (p, flip(c, k), h))

    def part_arrival(k, b):
        return remote(psrc.at[k, b], pdst.at[k, b], qs_sem.at[k, b], qr_sem.at[k, b], (p, c, other))

    for k in [k for k in reversed(order)]:
        n = order.index(k)
        for h in range(2):
            psrc[k, h] = pacc[:, n * genes + h * half:n * genes + (h + 1) * half]
            if k:
                part_copy(k, h).start()
    part_copy(0, other).start()
    total = psrc[0, l] - 1.0 / 8
    part_arrival(0, other).wait_recv()
    total = total + pdst[0, other]
    for k in range(1, cols):
        for b in range(2):
            part_arrival(k, b).wait_recv()
            total = total + pdst[k, b]

    def back_arrival(j):
        return remote(rsrc.at[0], rdst.at[j], ts_sem.at[0], tr_sem.at[j], (p, c, other))

    n_back = by_row([len(back[q]) for q in range(rows)])
    least = min(len(back[q]) for q in range(rows))
    for j in range(least):
        back_arrival(j).wait_recv()
        total = total + rdst[j]
    psrc[0, l] = total
    for j in range(least, max(len(back[q]) for q in range(rows))):
        @pl.when(n_back > j)
        def _():
            back_arrival(j).wait_recv()
            psrc[0, l] += rdst[j]
    out_ref[...] = jnp.sum(psrc[0, l], axis=0)

    exchange.wait_send()
    for k, s in panel_copies:
        panel_copies[k, s].wait_send()
        forward(k, s).wait_send()
    for k in range(1, cols):
        for h in range(2):
            part_copy(k, h).wait_send()
    part_copy(0, other).wait_send()
    for q in range(rows):
        @pl.when(p == q)
        def _():
            for f in outs[q]:
                for h in range(2):
                    for i in range(2):
                        z_copy(f, h, i).wait_send()
            for f in relays:
                if f[2] == q:
                    for b in range(2):
                        for i in range(2):
                            relay_copy(f, b, i).wait_send()
            for f in slots[q]:
                back_copy(f).wait_send()


def solution(mesh):
    rows, cols = mesh.shape["row"], mesh.shape["col"]
    flows = plan(rows)
    depth = max(len([f for f in flows if f[1] == q]) for q in range(rows))
    fan = max(len([f for f in flows if f[0] == q]) for q in range(rows))
    dma = lambda *shape: pltpu.SemaphoreType.DMA(shape)

    def on_device(expression):
        genes, part = expression.shape
        half, samples = genes // 2, 2 * part
        bf16, f32 = jnp.bfloat16, jnp.float32
        summed = pl.pallas_call(
            functools.partial(kernel, rows, cols),
            out_shape=jax.ShapeDtypeStruct((half,), f32),
            in_specs=[pl.BlockSpec(memory_space=pl.ANY)],
            out_specs=pl.BlockSpec(memory_space=pltpu.VMEM),
            scratch_shapes=[
                pltpu.VMEM((cols, 2, genes, part), bf16),
                pltpu.VMEM((cols * genes, samples), bf16),
                pltpu.VMEM((depth, 2, half, part), bf16),
                pltpu.VMEM((depth, half, samples), bf16),
                pltpu.VMEM((8, cols * genes), f32),
                pltpu.VMEM((depth, half, 128), f32),
                pltpu.VMEM((cols, 2, 8, half), f32),
                pltpu.VMEM((cols, 2, 8, half), f32),
                pltpu.VMEM((depth, 8, half), f32),
                pltpu.VMEM((fan, 8, half), f32),
                pltpu.SemaphoreType.DMA,
                dma(2),
                dma(cols - 1, 2), dma(cols - 1, 2),
                dma(cols - 1, 2), dma(cols - 1, 2),
                dma(fan, 2, 2), dma(depth, 2, 2),
                dma(2, 2),
                dma(cols, 2), dma(cols, 2),
                dma(depth), dma(fan),
                pltpu.SemaphoreType.REGULAR((cols - 1,)),
                pltpu.SemaphoreType.REGULAR((fan,)),
            ],
            compiler_params=pltpu.CompilerParams(collective_id=0, has_side_effects=True, vmem_limit_bytes=48000000),
        )(pltpu.with_memory_space_constraint(expression, pltpu.HBM))
        return summed

    return jax.shard_map(
        on_device,
        mesh=mesh,
        in_specs=(P(("row", "col"), "layer"),),
        out_specs=P(("row", "col", "layer")),
        check_vma=False,
    )
```

time: 31 us -> 29.5 us (0.952)
  Pallas kernels: 30.3 us -> 28.8 us
    pallas_call x1, Pallas kernels: 30.3 us -> 28.8 us  [on_device(): pl.pallas_call(functools.partial(kernel, rows, cols), out_shape=jax.Shape...]
where the time goes in v2:
time: 29.5 us; the launch traced here: 29.4 us
  Pallas kernels  28.8 us (98%)
  local copies, waits for them, and re-layouts  0.56 us (2%)
    pallas_call x1, Pallas kernels, on_device(): pl.pallas_call(functools.partial(kernel, rows, cols), out_shape=jax.Shape...  28.8 us

profile of v2, /device:TPU:0, one launch (start us, length us, event | category | flops | bytes accessed | tf_op | source)
XLA Modules:
  0.0 29.4 jit_solution(15486667483929743127)
XLA Ops:
  0.0 28.8 %shard_map.17 = f32[192]{0:T(256)S(1)} custom-call(bf16[384,512]{1,0:T(8,128)(2,1)} %x_ref.1), custom_call_target="tpu_custom_call" | custom-call | tf_op jit(solution)/shard_map/pallas_call | solution.py:399
  28.8 0.6 %copy.3 = f32[192]{0:T(256)} copy(f32[192]{0:T(256)S(1)} %shard_map.17) | data formatting | bytes 1536

commit v3 on v2

--- a/solution.py
+++ b/solution.py
@@ -27,7 +27,7 @@
 
 def plan(rows):
     if rows == 4:
-        return [(1, 0, None), (3, 1, None), (3, 0, 1), (0, 2, None), (1, 2, None), (2, 3, None)]
+        return [(3, 1, None), (0, 1, None), (3, 0, 1), (1, 2, None), (0, 2, 1), (2, 3, None)]
     flows = []
     for d in range(1, rows // 2 + 1):
         for s in range(rows if 2 * d < rows else rows // 2):
@@ -35,7 +35,7 @@
     return flows
 
 
-def kernel(rows, cols, x_ref, out_ref, praw, panel, far_raw, far, pacc, racc, psrc, pdst, rsrc, rdst,
+def kernel(rows, cols, x_ref, out_ref, praw, panel, far_raw, stack, pacc, racc, psrc, pdst, rsrc, rdst,
            in_sem, ex_sem, ps_sem, pr_sem, fs_sem, fr_sem, zs_sem, zr_sem, xs_sem, qs_sem, qr_sem, ts_sem, tr_sem,
            x_ready, z_ready):
     p, c, l = lax.axis_index("row"), lax.axis_index("col"), lax.axis_index("layer")
@@ -186,92 +186,107 @@
         gain = lax.rsqrt(variance + epsilon)
         return (((low - average) * gain).astype(jnp.bfloat16), ((high - average) * gain).astype(jnp.bfloat16))
 
-    def standardize(k):
+    def standardize(k, s):
         n = order.index(k)
-        for i in range(genes // step):
-            low, high = scale(praw[n, 0, pl.ds(i * step, step), :], praw[n, 1, pl.ds(i * step, step), :])
-            at = pl.ds(n * genes + i * step, step)
+        for i in range(half // step):
+            at = pl.ds(s * half + i * step, step)
+            low, high = scale(praw[n, 0, at, :], praw[n, 1, at, :])
+            at = pl.ds(n * genes + s * half + i * step, step)
             panel[at, 0:part] = low
             panel[at, part:samples] = high
 
-    def standardize_far(t, i):
-        for j in range(piece // step):
-            at = pl.ds(pl.multiple_of(i * piece + j * step, step), step)
+    def slot_at(t):
+        return (1 + t) * half
+
+    def standardize_far(t, first, stop):
+        for j in range(first // step, stop // step):
+            at = pl.ds(j * step, step)
             low, high = scale(far_raw[t, 0, at, :], far_raw[t, 1, at, :])
-            far[t, at, 0:part] = low
-            far[t, at, part:samples] = high
-
-    def adjacency(block, start, stop):
+            at = pl.ds(slot_at(t) + j * step, step)
+            stack[at, 0:part] = low
+            stack[at, part:samples] = high
+
+    def pairs(first, stop, start, end):
         product = lax.dot_general(
-            block, panel[start * genes:stop * genes, :], (((1,), (1,)), ((), ())), preferred_element_type=jnp.float32
+            stack[first:stop, :], panel[start * genes:end * genes, :], (((1,), (1,)), ((), ())),
+            preferred_element_type=jnp.float32
         )
         shifted = product * (0.5 / samples) + 0.5
         square = shifted * shifted
         fourth = square * square
         eighth = fourth * fourth
-        return eighth * fourth
-
-    def own_pairs(start, stop):
-        at = pl.ds(pl.multiple_of(l * half, half), half)
-        value = adjacency(panel[at, :], start, stop)
-        pacc[:, start * genes:stop * genes] += jnp.sum(value.reshape(half // 8, 8, value.shape[1]), axis=0)
-
-    def far_pairs(t, i, start, stop):
-        at = pl.ds(pl.multiple_of(i * piece, piece), piece)
-        value = adjacency(far[t, at, :], start, stop)
-        pacc[:, start * genes:stop * genes] += jnp.sum(value.reshape(piece // 8, 8, value.shape[1]), axis=0)
-        lanes = value[:, 0:128]
-        for j in range(1, value.shape[1] // 128):
-            lanes = lanes + value[:, j * 128:(j + 1) * 128]
-        racc[t, at, :] += lanes
+        value = eighth * fourth
+        width = value.shape[1]
+        pacc[:, start * genes:end * genes] += jnp.sum(value.reshape((stop - first) // 8, 8, width), axis=0)
+        skipped = max(half - first, 0)
+        if first + skipped < stop:
+            value = value[skipped:]
+            lanes = value[:, 0:128]
+            for j in range(1, width // 128):
+                lanes = lanes + value[:, j * 128:(j + 1) * 128]
+            racc[first + skipped - half:stop - half, :] += lanes
 
     exchange.wait_recv()
-    standardize(0)
-    own_pairs(0, 1)
+    for s in range(2):
+        standardize(0, s)
+    stack[0:half, :] = panel[pl.ds(pl.multiple_of(l * half, half), half), :]
+    pairs(0, half, 0, 1)
 
     relays = [f for f in flows if f[2] is not None]
 
+    def passed(f):
+        return slots[f[2]].index((f[0], f[2], None))
+
     def relay_copy(f, b, i):
-        t = slots[f[2]].index((f[0], f[2], None))
-        at = pl.ds(i * piece, piece)
-        return remote(far_raw.at[t, b, at], far_raw.at[slots[f[1]].index(f), b, at],
-                      xs_sem.at[b, i], zr_sem.at[slots[f[1]].index(f), b, i], (f[1], c, l))
-
-    def relay(i):
-        for f in relays:
+        at, t = pl.ds(i * piece, piece), slots[f[1]].index(f)
+        return remote(far_raw.at[passed(f), b, at], far_raw.at[t, b, at],
+                      xs_sem.at[relays.index(f), b, i], zr_sem.at[t, b, i], (f[1], c, l))
+
+    def relay(n, i):
+        for f in relays[n:n + 1]:
             @pl.when(p == f[2])
             def _():
                 for b in range(2):
-                    z_arrival(slots[f[2]].index((f[0], f[2], None)), b, i).wait_recv()
+                    z_arrival(passed(f), b, i).wait_recv()
                     relay_copy(f, b, i).start()
 
+    relay(1, 0)
     for s in range(2):
         panel_copies[2 - s, s].wait_recv()
         panel_copies[3, s].start()
         forward(2 - s, s).start()
-    relay(0)
+    relay(0, 0)
+    for s in range(2):
+        forward(2 - s, s).wait_recv()
+        standardize(2 - s, s)
+    relay(1, 1)
+    for f in flows:
+        if held_back(f):
+            @pl.when(p == f[0])
+            def _():
+                for h in range(2):
+                    z_copy(f, h, 1).start()
     for s in range(2):
         panel_copies[1 + s, s].wait_recv()
         forward(1 + s, s).start()
+    relay(0, 1)
+    for s in range(2):
+        forward(1 + s, s).wait_recv()
+        standardize(1 + s, s)
     for k in direct[2:]:
         for s in range(2):
             panel_copies[k, s].wait_recv()
             forward(k, s).start()
-    relay(1)
-    for f in flows:
-        if held_back(f):
-            @pl.when(p == f[0])
-            def _():
-                for h in range(2):
-                    z_copy(f, h, 1).start()
-    for k in direct:
         for s in range(2):
             forward(k, s).wait_recv()
-        standardize(k)
-    own_pairs(1, last)
+            standardize(k, s)
+    pairs(0, half, 1, last)
+    for s in range(2):
+        panel_copies[3, s].wait_recv()
+        forward(3, s).start()
 
     def take_far(t, i):
-        passing = [f[2] for f in relays if slots[f[2]].index((f[0], f[2], None)) == t]
+        passing = [f[2] for f in relays if passed(f) == t]
         if passing:
             @pl.when(p != passing[0])
             def _():
@@ -280,10 +295,13 @@
         else:
             for b in range(2):
                 z_arrival(t, b, i).wait_recv()
-        standardize_far(t, i)
+
+    def back_copy(f):
+        t, j = slots[f[1]].index(f), back[f[0]].index(f)
+        return remote(rsrc.at[t], rdst.at[j], ts_sem.at[t], tr_sem.at[j], (f[0], c, l))
 
     def give_back(t):
-        turned = racc[t].T
+        turned = racc[t * half:(t + 1) * half, :].T
         rsrc[t] = jnp.sum(turned.reshape(128 // 8, 8, half), axis=0)
         for q in range(rows):
             if t < len(slots[q]):
@@ -291,38 +309,33 @@
                 def _():
                     back_copy(slots[q][t]).start()
 
-    def back_copy(f):
-        t, j = slots[f[1]].index(f), back[f[0]].index(f)
-        return remote(rsrc.at[t], rdst.at[j], ts_sem.at[t], tr_sem.at[j], (f[0], c, l))
-
-    @pl.loop(0, 2)
-    def _(i):
-        take_far(0, i)
-        far_pairs(0, i, 0, last)
-
-    for s in range(2):
-        panel_copies[3, s].wait_recv()
-        forward(3, s).start()
+    depth = max(len(slots[q]) for q in range(rows))
+    n_slots = by_row([len(slots[q]) for q in range(rows)])
+    for t in range(1, depth):
+        @pl.when(n_slots > t)
+        def _():
+            for i in range(2):
+                take_far(t, i)
+            standardize_far(t, 0, half)
+            pairs(slot_at(t), slot_at(t) + half, 0, last)
+
+    take_far(0, 0)
+    standardize_far(0, 0, piece)
+    pairs(half, half + piece, 0, last)
     for s in range(2):
         forward(3, s).wait_recv()
-    standardize(3)
-    own_pairs(last, cols)
-
-    @pl.loop(0, 2)
-    def _(i):
-        far_pairs(0, i, last, cols)
-
+        standardize(3, s)
+    pairs(0, half + piece, last, cols)
+    for t in range(1, depth):
+        @pl.when(n_slots > t)
+        def _():
+            pairs(slot_at(t), slot_at(t) + half, last, cols)
+            give_back(t)
+
+    take_far(0, 1)
+    standardize_far(0, piece, half)
+    pairs(half + piece, 2 * half, 0, cols)
     give_back(0)
-    depth = max(len(slots[q]) for q in range(rows))
-    for t in range(1, depth):
-        @pl.when(by_row([len(slots[q]) for q in range(rows)]) > t)
-        def _():
-            @pl.loop(0, 2)
-            def _(i):
-                take_far(t, i)
-                far_pairs(t, i, 0, cols)
-
-            give_back(t)
 
     def part_copy(k, h):
         return remote(psrc.at[k, h], pdst.at[k, l], qs_sem.at[k, h], qr_sem.at[k, l], (p, flip(c, k), h))
@@ -405,9 +418,9 @@
                 pltpu.VMEM((cols, 2, genes, part), bf16),
                 pltpu.VMEM((cols * genes, samples), bf16),
                 pltpu.VMEM((depth, 2, half, part), bf16),
-                pltpu.VMEM((depth, half, samples), bf16),
+                pltpu.VMEM(((1 + depth) * half, samples), bf16),
                 pltpu.VMEM((8, cols * genes), f32),
-                pltpu.VMEM((depth, half, 128), f32),
+                pltpu.VMEM((depth * half, 128), f32),
                 pltpu.VMEM((cols, 2, 8, half), f32),
                 pltpu.VMEM((cols, 2, 8, half), f32),
                 pltpu.VMEM((depth, 8, half), f32),
@@ -417,7 +430,7 @@
                 dma(cols - 1, 2), dma(cols - 1, 2),
                 dma(cols - 1, 2), dma(cols - 1, 2),
                 dma(fan, 2, 2), dma(depth, 2, 2),
-                dma(2, 2),
+                dma(max(len([f for f in flows if f[2] is not None]), 1), 2, 2),
                 dma(cols, 2), dma(cols, 2),
                 dma(depth), dma(fan),
                 pltpu.SemaphoreType.REGULAR((cols - 1,)),

time: 29.5 us -> 28.1 us (0.953)
  Pallas kernels: 28.8 us -> 27.4 us
    pallas_call x1, Pallas kernels: 28.8 us -> 27.4 us  [on_device(): pl.pallas_call(functools.partial(kernel, rows, cols), out_shape=jax.Shape...]
where the time goes in v3:
time: 28.1 us; the launch traced here: 28 us
  Pallas kernels  27.4 us (98%)
  local copies, waits for them, and re-layouts  0.56 us (2%)
    pallas_call x1, Pallas kernels, on_device(): pl.pallas_call(functools.partial(kernel, rows, cols), out_shape=jax.Shape...  27.4 us
    unnamed x1, local copies, waits for them, and re-layouts  0.56 us

profile of v3, /device:TPU:0, one launch (start us, length us, event | category | flops | bytes accessed | tf_op | source)
XLA Modules:
  0.0 28.0 jit_solution(10916548937341060692)
XLA Ops:
  0.0 27.4 %shard_map.17 = f32[192]{0:T(256)S(1)} custom-call(bf16[384,512]{1,0:T(8,128)(2,1)} %x_ref.1), custom_call_target="tpu_custom_call" | custom-call | tf_op jit(solution)/shard_map/pallas_call | solution.py:412
  27.4 0.6 %copy.3 = f32[192]{0:T(256)} copy(f32[192]{0:T(256)S(1)} %shard_map.17) | data formatting | bytes 1536

commit v4 on v3

--- a/solution.py
+++ b/solution.py
@@ -41,12 +41,15 @@
     p, c, l = lax.axis_index("row"), lax.axis_index("col"), lax.axis_index("layer")
     genes, part = x_ref.shape
     half = genes // 2
-    piece = half // 2
+    cuts = 4
+    piece = half // cuts
     samples = 2 * part
     other = 1 - l
     order = [k for k in range(cols) if k != 3] + [3]
     direct = [k for k in range(1, cols) if k != 3]
     last = cols - 1
+    places = [(0, 0), (0, 1), (1, 1), (2, 0), (1, 0), (2, 1)] + [(k, s) for k in order[3:] for s in range(2)]
+    ends = len(places)
     flows = plan(rows)
     slots = {t: [f for f in flows if f[1] == t] for t in range(rows)}
     outs = {s: [f for f in flows if f[0] == s and f[2] is None] for s in range(rows)}
@@ -122,7 +125,7 @@
         return rows == 4 and f == (1, 2, None)
 
     def send_row(f):
-        for i in range(1 if held_back(f) else 2):
+        for i in range(cuts // 2 if held_back(f) else cuts):
             for h in range(2):
                 z_copy(f, h, i).start()
 
@@ -187,11 +190,11 @@
         return (((low - average) * gain).astype(jnp.bfloat16), ((high - average) * gain).astype(jnp.bfloat16))
 
     def standardize(k, s):
-        n = order.index(k)
+        n, place = order.index(k), places.index((k, s))
         for i in range(half // step):
             at = pl.ds(s * half + i * step, step)
             low, high = scale(praw[n, 0, at, :], praw[n, 1, at, :])
-            at = pl.ds(n * genes + s * half + i * step, step)
+            at = pl.ds(place * half + i * step, step)
             panel[at, 0:part] = low
             panel[at, part:samples] = high
 
@@ -208,7 +211,7 @@
 
     def pairs(first, stop, start, end):
         product = lax.dot_general(
-            stack[first:stop, :], panel[start * genes:end * genes, :], (((1,), (1,)), ((), ())),
+            stack[first:stop, :], panel[start * half:end * half, :], (((1,), (1,)), ((), ())),
             preferred_element_type=jnp.float32
         )
         shifted = product * (0.5 / samples) + 0.5
@@ -217,7 +220,7 @@
         eighth = fourth * fourth
         value = eighth * fourth
         width = value.shape[1]
-        pacc[:, start * genes:end * genes] += jnp.sum(value.reshape((stop - first) // 8, 8, width), axis=0)
+        pacc[:, start * half:end * half] += jnp.sum(value.reshape((stop - first) // 8, 8, width), axis=0)
         skipped = max(half - first, 0)
         if first + skipped < stop:
             value = value[skipped:]
@@ -230,7 +233,7 @@
     for s in range(2):
         standardize(0, s)
     stack[0:half, :] = panel[pl.ds(pl.multiple_of(l * half, half), half), :]
-    pairs(0, half, 0, 1)
+    pairs(0, half, 0, 2)
 
     relays = [f for f in flows if f[2] is not None]
 
@@ -250,26 +253,76 @@
                     z_arrival(passed(f), b, i).wait_recv()
                     relay_copy(f, b, i).start()
 
-    relay(1, 0)
+    for n, i in [(1, 0), (1, 1), (0, 0)]:
+        relay(n, i)
     for s in range(2):
         panel_copies[2 - s, s].wait_recv()
         panel_copies[3, s].start()
         forward(2 - s, s).start()
-    relay(0, 0)
+    for n, i in [(0, 1), (1, 2)]:
+        relay(n, i)
     for s in range(2):
         forward(2 - s, s).wait_recv()
         standardize(2 - s, s)
-    relay(1, 1)
+    pairs(0, half, 2, 4)
+    for n, i in [(1, 3), (0, 2)]:
+        relay(n, i)
     for f in flows:
         if held_back(f):
             @pl.when(p == f[0])
             def _():
-                for h in range(2):
-                    z_copy(f, h, 1).start()
+                for i in range(cuts // 2, cuts):
+                    for h in range(2):
+                        z_copy(f, h, i).start()
     for s in range(2):
         panel_copies[1 + s, s].wait_recv()
         forward(1 + s, s).start()
-    relay(0, 1)
+    relay(0, 3)
+
+    def take_far(t, i):
+        passing = [f[2] for f in relays if passed(f) == t]
+        if passing:
+            @pl.when(p != passing[0])
+            def _():
+                for b in range(2):
+                    z_arrival(t, b, i).wait_recv()
+        else:
+            for b in range(2):
+                z_arrival(t, b, i).wait_recv()
+
+    def back_copy(f):
+        t, j = slots[f[1]].index(f), back[f[0]].index(f)
+        return remote(rsrc.at[t], rdst.at[j], ts_sem.at[t], tr_sem.at[j], (f[0], c, l))
+
+    def give_back(t):
+        turned = racc[t * half:(t + 1) * half, :].T
+        rsrc[t] = jnp.sum(turned.reshape(128 // 8, 8, half), axis=0)
+        for q in range(rows):
+            if t < len(slots[q]):
+                @pl.when(p == q)
+                def _():
+                    back_copy(slots[q][t]).start()
+
+    depth = max(len(slots[q]) for q in range(rows))
+    n_slots = by_row([len(slots[q]) for q in range(rows)])
+    middle = half + half // 2
+
+    def take_block(t):
+        for i in range(cuts):
+            take_far(t, i)
+        standardize_far(t, 0, half)
+
+    soon = by_row([2 if any(f[2] == q for f in flows) else 1 for q in range(rows)])
+    for i in range(cuts // 2):
+        take_far(0, i)
+    standardize_far(0, 0, half // 2)
+    pairs(half, middle, 0, 4)
+    for t in range(1, depth):
+        @pl.when(jnp.minimum(n_slots, soon) > t)
+        def _():
+            take_block(t)
+            pairs(slot_at(t), slot_at(t) + half, 0, 4)
+
     for s in range(2):
         forward(1 + s, s).wait_recv()
         standardize(1 + s, s)
@@ -280,62 +333,35 @@
         for s in range(2):
             forward(k, s).wait_recv()
             standardize(k, s)
-    pairs(0, half, 1, last)
+    pairs(0, middle, 4, ends - 2)
     for s in range(2):
         panel_copies[3, s].wait_recv()
         forward(3, s).start()
-
-    def take_far(t, i):
-        passing = [f[2] for f in relays if passed(f) == t]
-        if passing:
-            @pl.when(p != passing[0])
-            def _():
-                for b in range(2):
-                    z_arrival(t, b, i).wait_recv()
-        else:
-            for b in range(2):
-                z_arrival(t, b, i).wait_recv()
-
-    def back_copy(f):
-        t, j = slots[f[1]].index(f), back[f[0]].index(f)
-        return remote(rsrc.at[t], rdst.at[j], ts_sem.at[t], tr_sem.at[j], (f[0], c, l))
-
-    def give_back(t):
-        turned = racc[t * half:(t + 1) * half, :].T
-        rsrc[t] = jnp.sum(turned.reshape(128 // 8, 8, half), axis=0)
-        for q in range(rows):
-            if t < len(slots[q]):
-                @pl.when(p == q)
-                def _():
-                    back_copy(slots[q][t]).start()
-
-    depth = max(len(slots[q]) for q in range(rows))
-    n_slots = by_row([len(slots[q]) for q in range(rows)])
     for t in range(1, depth):
         @pl.when(n_slots > t)
         def _():
-            for i in range(2):
-                take_far(t, i)
-            standardize_far(t, 0, half)
-            pairs(slot_at(t), slot_at(t) + half, 0, last)
-
-    take_far(0, 0)
-    standardize_far(0, 0, piece)
-    pairs(half, half + piece, 0, last)
+            @pl.when(soon > t)
+            def _():
+                pairs(slot_at(t), slot_at(t) + half, 4, ends - 2)
+
+            @pl.when(soon <= t)
+            def _():
+                take_block(t)
+                pairs(slot_at(t), slot_at(t) + half, 0, ends - 2)
+
     for s in range(2):
         forward(3, s).wait_recv()
         standardize(3, s)
-    pairs(0, half + piece, last, cols)
+    pairs(0, middle, ends - 2, ends)
     for t in range(1, depth):
         @pl.when(n_slots > t)
         def _():
-            pairs(slot_at(t), slot_at(t) + half, last, cols)
+            pairs(slot_at(t), slot_at(t) + half, ends - 2, ends)
             give_back(t)
 
-    take_far(0, 1)
-    standardize_far(0, piece, half)
-    pairs(half + piece, 2 * half, 0, cols)
-    give_back(0)
+    for i in range(cuts // 2, cuts):
+        take_far(0, i)
+    standardize_far(0, half // 2, half)
 
     def part_copy(k, h):
         return remote(psrc.at[k, h], pdst.at[k, l], qs_sem.at[k, h], qr_sem.at[k, l], (p, flip(c, k), h))
@@ -343,13 +369,22 @@
     def part_arrival(k, b):
         return remote(psrc.at[k, b], pdst.at[k, b], qs_sem.at[k, b], qr_sem.at[k, b], (p, c, other))
 
-    for k in [k for k in reversed(order)]:
-        n = order.index(k)
+    def send_parts(k):
         for h in range(2):
-            psrc[k, h] = pacc[:, n * genes + h * half:n * genes + (h + 1) * half]
+            place = places.index((k, h))
+            psrc[k, h] = pacc[:, place * half:(place + 1) * half]
             if k:
                 part_copy(k, h).start()
+
+    pairs(middle, 2 * half, ends - 2, ends)
+    send_parts(3)
+    pairs(middle, 2 * half, 2, ends - 2)
+    for k in direct:
+        send_parts(k)
+    pairs(middle, 2 * half, 0, 2)
+    send_parts(0)
     part_copy(0, other).start()
+    give_back(0)
     total = psrc[0, l] - 1.0 / 8
     part_arrival(0, other).wait_recv()
     total = total + pdst[0, other]
@@ -387,12 +422,12 @@
         def _():
             for f in outs[q]:
                 for h in range(2):
-                    for i in range(2):
+                    for i in range(cuts):
                         z_copy(f, h, i).wait_send()
             for f in relays:
                 if f[2] == q:
                     for b in range(2):
-                        for i in range(2):
+                        for i in range(cuts):
                             relay_copy(f, b, i).wait_send()
             for f in slots[q]:
                 back_copy(f).wait_send()
@@ -429,8 +464,8 @@
                 dma(2),
                 dma(cols - 1, 2), dma(cols - 1, 2),
                 dma(cols - 1, 2), dma(cols - 1, 2),
-                dma(fan, 2, 2), dma(depth, 2, 2),
-                dma(max(len([f for f in flows if f[2] is not None]), 1), 2, 2),
+                dma(fan, 2, 4), dma(depth, 2, 4),
+                dma(max(len([f for f in flows if f[2] is not None]), 1), 2, 4),
                 dma(cols, 2), dma(cols, 2),
                 dma(depth), dma(fan),
                 pltpu.SemaphoreType.REGULAR((cols - 1,)),

time: 28.1 us -> 26.7 us (0.950)
  Pallas kernels: 27.4 us -> 25.9 us
    pallas_call x1, Pallas kernels: 27.4 us -> 25.9 us  [on_device(): pl.pallas_call(functools.partial(kernel, rows, cols), out_shape=jax.Shape...]
where the time goes in v4:
time: 26.7 us; the launch traced here: 26.5 us
  Pallas kernels  25.9 us (97%)
  local copies, waits for them, and re-layouts  0.56 us (2%)
    pallas_call x1, Pallas kernels, on_device(): pl.pallas_call(functools.partial(kernel, rows, cols), out_shape=jax.Shape...  25.9 us
    unnamed x1, local copies, waits for them, and re-layouts  0.56 us

profile of v4, /device:TPU:0, one launch (start us, length us, event | category | flops | bytes accessed | tf_op | source)
XLA Modules:
  0.0 26.5 jit_solution(6041979436432854186)
XLA Ops:
  0.0 25.9 %shard_map.17 = f32[192]{0:T(256)S(1)} custom-call(bf16[384,512]{1,0:T(8,128)(2,1)} %x_ref.1), custom_call_target="tpu_custom_call" | custom-call | tf_op jit(solution)/shard_map/pallas_call | solution.py:447
  25.9 0.6 %copy.3 = f32[192]{0:T(256)} copy(f32[192]{0:T(256)S(1)} %shard_map.17) | data formatting | bytes 1536

commit v5 on v4

--- a/solution.py
+++ b/solution.py
@@ -35,7 +35,7 @@
     return flows
 
 
-def kernel(rows, cols, x_ref, out_ref, praw, panel, far_raw, stack, pacc, racc, psrc, pdst, rsrc, rdst,
+def kernel(rows, cols, x_ref, out_ref, praw, panel, across, far_raw, stack, pacc, racc, psrc, pdst, rsrc, rdst,
            in_sem, ex_sem, ps_sem, pr_sem, fs_sem, fr_sem, zs_sem, zr_sem, xs_sem, qs_sem, qr_sem, ts_sem, tr_sem,
            x_ready, z_ready):
     p, c, l = lax.axis_index("row"), lax.axis_index("col"), lax.axis_index("layer")
@@ -78,7 +78,12 @@
     def greet(device):
         pl.semaphore_signal(barrier, inc=1, device_id=device, device_id_type=MESH)
 
-    greet((p, c, other))
+    alone = jnp.logical_and(p == 0, c == 0)
+
+    @pl.when(jnp.logical_or(alone, l == 1))
+    def _():
+        greet((p, c, other))
+
     for k in direct:
         @pl.when(is_above(c, k))
         def _():
@@ -91,7 +96,7 @@
                 for t in above:
                     for h in range(2):
                         greet((t, c, h))
-    greetings = 1 + by_row([2 * len([t for t in pairs_of[q] if t < q]) for q in range(rows)])
+    greetings = jnp.where(alone, 1, other) + by_row([2 * len([t for t in pairs_of[q] if t < q]) for q in range(rows)])
     for k in direct:
         greetings = greetings + jnp.where(is_above(c, k), 0, 1)
 
@@ -109,7 +114,12 @@
             def _():
                 for f in below:
                     for h in range(2):
-                        pl.semaphore_signal(z_ready.at[outs[f[0]].index(f)], inc=1, device_id=(f[0], c, h), device_id_type=MESH)
+                        pl.semaphore_signal(z_ready.at[outs[f[0]].index(f), l], inc=1, device_id=(f[0], c, h), device_id_type=MESH)
+
+    @pl.when(l == 0)
+    def _():
+        pl.semaphore_signal(x_ready.at[2], inc=1, device_id=(p, c, other), device_id_type=MESH)
+
     load.wait()
 
     def z_copy(f, h, i):
@@ -124,12 +134,19 @@
     def held_back(f):
         return rows == 4 and f == (1, 2, None)
 
-    def send_row(f):
+    def send_row(f, ask=False):
         for i in range(cuts // 2 if held_back(f) else cuts):
-            for h in range(2):
+            for h in (1, 0):
+                if ask and i == 0:
+                    pl.semaphore_wait(z_ready.at[outs[f[0]].index(f), h], 1)
                 z_copy(f, h, i).start()
 
     exchange = remote(praw.at[0, l], praw.at[0, l], ex_sem.at[0], ex_sem.at[1], (p, c, other))
+
+    @pl.when(l == 1)
+    def _():
+        pl.semaphore_wait(x_ready.at[2], 1)
+
     exchange.start()
     for q in range(rows):
         down = [f for f in outs[q] if f[1] < q]
@@ -175,8 +192,7 @@
             @pl.when(p == q)
             def _():
                 for f in up:
-                    pl.semaphore_wait(z_ready.at[outs[q].index(f)], 2)
-                    send_row(f)
+                    send_row(f, ask=True)
 
     step = 32
 
@@ -209,11 +225,18 @@
             stack[at, 0:part] = low
             stack[at, part:samples] = high
 
-    def pairs(first, stop, start, end):
-        product = lax.dot_general(
-            stack[first:stop, :], panel[start * half:end * half, :], (((1,), (1,)), ((), ())),
-            preferred_element_type=jnp.float32
-        )
+    def turn(start, end):
+        for at in range(start * half, end * half, 128):
+            across[:, at:at + 128] = panel[at:at + 128, :].T
+
+    def pairs(first, stop, start, end, turned=False):
+        if turned:
+            product = jnp.dot(stack[first:stop, :], across[:, start * half:end * half], preferred_element_type=jnp.float32)
+        else:
+            product = lax.dot_general(
+                stack[first:stop, :], panel[start * half:end * half, :], (((1,), (1,)), ((), ())),
+                preferred_element_type=jnp.float32
+            )
         shifted = product * (0.5 / samples) + 0.5
         square = shifted * shifted
         fourth = square * square
@@ -234,6 +257,7 @@
         standardize(0, s)
     stack[0:half, :] = panel[pl.ds(pl.multiple_of(l * half, half), half), :]
     pairs(0, half, 0, 2)
+    turn(0, 2)
 
     relays = [f for f in flows if f[2] is not None]
 
@@ -253,7 +277,7 @@
                     z_arrival(passed(f), b, i).wait_recv()
                     relay_copy(f, b, i).start()
 
-    for n, i in [(1, 0), (1, 1), (0, 0)]:
+    for n, i in [(1, 0), (0, 0), (1, 1)]:
         relay(n, i)
     for s in range(2):
         panel_copies[2 - s, s].wait_recv()
@@ -265,6 +289,7 @@
         forward(2 - s, s).wait_recv()
         standardize(2 - s, s)
     pairs(0, half, 2, 4)
+    turn(2, 4)
     for n, i in [(1, 3), (0, 2)]:
         relay(n, i)
     for f in flows:
@@ -272,7 +297,7 @@
             @pl.when(p == f[0])
             def _():
                 for i in range(cuts // 2, cuts):
-                    for h in range(2):
+                    for h in (1, 0):
                         z_copy(f, h, i).start()
     for s in range(2):
         panel_copies[1 + s, s].wait_recv()
@@ -316,12 +341,12 @@
     for i in range(cuts // 2):
         take_far(0, i)
     standardize_far(0, 0, half // 2)
-    pairs(half, middle, 0, 4)
+    pairs(half, middle, 0, 4, True)
     for t in range(1, depth):
         @pl.when(jnp.minimum(n_slots, soon) > t)
         def _():
             take_block(t)
-            pairs(slot_at(t), slot_at(t) + half, 0, 4)
+            pairs(slot_at(t), slot_at(t) + half, 0, 4, True)
 
     for s in range(2):
         forward(1 + s, s).wait_recv()
@@ -337,17 +362,18 @@
     for s in range(2):
         panel_copies[3, s].wait_recv()
         forward(3, s).start()
+    turn(4, ends - 2)
     for t in range(1, depth):
         @pl.when(n_slots > t)
         def _():
             @pl.when(soon > t)
             def _():
-                pairs(slot_at(t), slot_at(t) + half, 4, ends - 2)
+                pairs(slot_at(t), slot_at(t) + half, 4, ends - 2, True)
 
             @pl.when(soon <= t)
             def _():
                 take_block(t)
-                pairs(slot_at(t), slot_at(t) + half, 0, ends - 2)
+                pairs(slot_at(t), slot_at(t) + half, 0, ends - 2, True)
 
     for s in range(2):
         forward(3, s).wait_recv()
@@ -359,6 +385,7 @@
             pairs(slot_at(t), slot_at(t) + half, ends - 2, ends)
             give_back(t)
 
+    turn(ends - 2, ends)
     for i in range(cuts // 2, cuts):
         take_far(0, i)
     standardize_far(0, half // 2, half)
@@ -376,12 +403,12 @@
             if k:
                 part_copy(k, h).start()
 
-    pairs(middle, 2 * half, ends - 2, ends)
+    pairs(middle, 2 * half, ends - 2, ends, True)
     send_parts(3)
-    pairs(middle, 2 * half, 2, ends - 2)
+    pairs(middle, 2 * half, 2, ends - 2, True)
     for k in direct:
         send_parts(k)
-    pairs(middle, 2 * half, 0, 2)
+    pairs(middle, 2 * half, 0, 2, True)
     send_parts(0)
     part_copy(0, other).start()
     give_back(0)
@@ -452,6 +479,7 @@
             scratch_shapes=[
                 pltpu.VMEM((cols, 2, genes, part), bf16),
                 pltpu.VMEM((cols * genes, samples), bf16),
+                pltpu.VMEM((samples, cols * genes), bf16),
                 pltpu.VMEM((depth, 2, half, part), bf16),
                 pltpu.VMEM(((1 + depth) * half, samples), bf16),
                 pltpu.VMEM((8, cols * genes), f32),
@@ -469,7 +497,7 @@
                 dma(cols, 2), dma(cols, 2),
                 dma(depth), dma(fan),
                 pltpu.SemaphoreType.REGULAR((cols - 1,)),
-                pltpu.SemaphoreType.REGULAR((fan,)),
+                pltpu.SemaphoreType.REGULAR((fan, 2)),
             ],
             compiler_params=pltpu.CompilerParams(collective_id=0, has_side_effects=True, vmem_limit_bytes=48000000),
         )(pltpu.with_memory_space_constraint(expression, pltpu.HBM))

time: 26.7 us -> 26.5 us (level)
  Pallas kernels: 25.9 us -> 25.6 us
    pallas_call x1, Pallas kernels: 25.9 us -> 25.6 us  [on_device(): pl.pallas_call(functools.partial(kernel, rows, cols), out_shape=jax.Shape...]
where the time goes in v5:
time: 26.5 us; the launch traced here: 26.2 us
  Pallas kernels  25.6 us (97%)
  local copies, waits for them, and re-layouts  0.56 us (2%)
    pallas_call x1, Pallas kernels, on_device(): pl.pallas_call(functools.partial(kernel, rows, cols), out_shape=jax.Shape...  25.6 us
    unnamed x1, local copies, waits for them, and re-layouts  0.56 us

profile of v5, /device:TPU:0, one launch (start us, length us, event | category | flops | bytes accessed | tf_op | source)
XLA Modules:
  0.0 26.2 jit_solution(5259000303455960497)
XLA Ops:
  0.0 25.6 %shard_map.17 = f32[192]{0:T(256)S(1)} custom-call(bf16[384,512]{1,0:T(8,128)(2,1)} %x_ref.1), custom_call_target="tpu_custom_call" | custom-call | tf_op jit(solution)/shard_map/pallas_call | solution.py:474
  25.6 0.6 %copy.3 = f32[192]{0:T(256)} copy(f32[192]{0:T(256)S(1)} %shard_map.17) | data formatting | bytes 1536

commit v6 on v5

--- a/solution.py
+++ b/solution.py
@@ -378,13 +378,13 @@
     for s in range(2):
         forward(3, s).wait_recv()
         standardize(3, s)
-    pairs(0, middle, ends - 2, ends)
     for t in range(1, depth):
         @pl.when(n_slots > t)
         def _():
             pairs(slot_at(t), slot_at(t) + half, ends - 2, ends)
             give_back(t)
 
+    pairs(0, middle, ends - 2, ends)
     turn(ends - 2, ends)
     for i in range(cuts // 2, cuts):
         take_far(0, i)
@@ -405,36 +405,20 @@
 
     pairs(middle, 2 * half, ends - 2, ends, True)
     send_parts(3)
-    pairs(middle, 2 * half, 2, ends - 2, True)
-    for k in direct:
+    pairs(middle, 2 * half, 0, ends - 2, True)
+    sums_first = p < rows // 2
+
+    @pl.when(jnp.logical_not(sums_first))
+    def _():
+        give_back(0)
+
+    for k in direct + [0]:
         send_parts(k)
-    pairs(middle, 2 * half, 0, 2, True)
-    send_parts(0)
     part_copy(0, other).start()
-    give_back(0)
-    total = psrc[0, l] - 1.0 / 8
-    part_arrival(0, other).wait_recv()
-    total = total + pdst[0, other]
-    for k in range(1, cols):
-        for b in range(2):
-            part_arrival(k, b).wait_recv()
-            total = total + pdst[k, b]
-
-    def back_arrival(j):
-        return remote(rsrc.at[0], rdst.at[j], ts_sem.at[0], tr_sem.at[j], (p, c, other))
-
-    n_back = by_row([len(back[q]) for q in range(rows)])
-    least = min(len(back[q]) for q in range(rows))
-    for j in range(least):
-        back_arrival(j).wait_recv()
-        total = total + rdst[j]
-    psrc[0, l] = total
-    for j in range(least, max(len(back[q]) for q in range(rows))):
-        @pl.when(n_back > j)
-        def _():
-            back_arrival(j).wait_recv()
-            psrc[0, l] += rdst[j]
-    out_ref[...] = jnp.sum(psrc[0, l], axis=0)
+
+    @pl.when(sums_first)
+    def _():
+        give_back(0)
 
     exchange.wait_send()
     for k, s in panel_copies:
@@ -458,6 +442,30 @@
                             relay_copy(f, b, i).wait_send()
             for f in slots[q]:
                 back_copy(f).wait_send()
+
+    total = psrc[0, l] - 1.0 / 8
+    part_arrival(0, other).wait_recv()
+    total = total + pdst[0, other]
+    for k in range(1, cols):
+        for b in range(2):
+            part_arrival(k, b).wait_recv()
+            total = total + pdst[k, b]
+
+    def back_arrival(j):
+        return remote(rsrc.at[0], rdst.at[j], ts_sem.at[0], tr_sem.at[j], (p, c, other))
+
+    n_back = by_row([len(back[q]) for q in range(rows)])
+    least = min(len(back[q]) for q in range(rows))
+    for j in range(least):
+        back_arrival(j).wait_recv()
+        total = total + rdst[j]
+    psrc[0, l] = total
+    for j in range(least, max(len(back[q]) for q in range(rows))):
+        @pl.when(n_back > j)
+        def _():
+            back_arrival(j).wait_recv()
+            psrc[0, l] += rdst[j]
+    out_ref[...] = jnp.sum(psrc[0, l], axis=0)
 
 
 def solution(mesh):

time: 26.5 us -> 26.4 us (level)
  the two profiles are of different devices: /device:TPU:0 before, /device:TPU:17 now
where the time goes in v6:
time: 26.4 us; the launch traced here: 26.3 us
  Pallas kernels  25.7 us (97%)
  local copies, waits for them, and re-layouts  0.56 us (2%)
    pallas_call x1, Pallas kernels, on_device(): pl.pallas_call(functools.partial(kernel, rows, cols), out_shape=jax.Shape...  25.7 us
    unnamed x1, local copies, waits for them, and re-layouts  0.56 us

profile of v6, /device:TPU:17, one launch (start us, length us, event | category | flops | bytes accessed | tf_op | source)
XLA Modules:
  0.0 26.3 jit_solution(10933534872207743390)
XLA Ops:
  0.0 25.7 %shard_map.17 = f32[192]{0:T(256)S(1)} custom-call(bf16[384,512]{1,0:T(8,128)(2,1)} %x_ref.1), custom_call_target="tpu_custom_call" | custom-call | tf_op jit(solution)/shard_map/pallas_call | solution.py:482
  25.7 0.6 %copy.3 = f32[192]{0:T(256)} copy(f32[192]{0:T(256)S(1)} %shard_map.17) | data formatting | bytes 1536

commit v7 on v6

--- a/solution.py
+++ b/solution.py
@@ -36,8 +36,8 @@
 
 
 def kernel(rows, cols, x_ref, out_ref, praw, panel, across, far_raw, stack, pacc, racc, psrc, pdst, rsrc, rdst,
-           in_sem, ex_sem, ps_sem, pr_sem, fs_sem, fr_sem, zs_sem, zr_sem, xs_sem, qs_sem, qr_sem, ts_sem, tr_sem,
-           x_ready, z_ready):
+           in_sem, ex_sem, own_sent, passed_sent, far_sent, parts_sent, back_sent,
+           pr_sem, fr_sem, zr_sem, parts_here, back_here, x_ready, z_ready):
     p, c, l = lax.axis_index("row"), lax.axis_index("col"), lax.axis_index("layer")
     genes, part = x_ref.shape
     half = genes // 2
@@ -56,6 +56,9 @@
     back = {s: [f for f in flows if f[0] == s] for s in range(rows)}
     pairs_of = {q: sorted({f[1] for f in flows if f[0] == q} | {f[0] for f in flows if f[1] == q}) for q in range(rows)}
 
+    def held_back(f):
+        return rows == 4 and f == (1, 2, None)
+
     def remote(src, dst, send, recv, device):
         return pltpu.make_async_remote_copy(
             src_ref=src, dst_ref=dst, send_sem=send, recv_sem=recv, device_id=device, device_id_type=MESH
@@ -87,37 +90,43 @@
     for k in direct:
         @pl.when(is_above(c, k))
         def _():
-            greet((p, flip(c, k), l))
+            for h in range(2):
+                greet((p, flip(c, k), h))
     for q in range(rows):
         above = [t for t in pairs_of[q] if t > q]
-        if above:
+        if above or any(held_back(f) for f in slots[q]):
             @pl.when(p == q)
             def _():
                 for t in above:
                     for h in range(2):
                         greet((t, c, h))
+                for f in slots[q]:
+                    if held_back(f):
+                        greet((f[0], c, 1))
     greetings = jnp.where(alone, 1, other) + by_row([2 * len([t for t in pairs_of[q] if t < q]) for q in range(rows)])
     for k in direct:
-        greetings = greetings + jnp.where(is_above(c, k), 0, 1)
-
+        greetings = greetings + jnp.where(is_above(c, k), 0, 2)
+
+    greetings = greetings + l * by_row([2 * len([f for f in outs[q] if held_back(f)]) for q in range(rows)])
     pacc[...] = jnp.zeros_like(pacc)
     racc[...] = jnp.zeros_like(racc)
     pl.semaphore_wait(barrier, greetings)
-    for k in direct:
-        @pl.when(jnp.logical_not(is_above(c, k)))
-        def _():
-            pl.semaphore_signal(x_ready.at[k - 1], inc=1, device_id=(p, flip(c, k), l), device_id_type=MESH)
-    for t in range(rows):
-        below = [f for f in slots[t] if f[2] is None and f[0] < t]
-        if below:
-            @pl.when(p == t)
-            def _():
-                for f in below:
-                    for h in range(2):
-                        pl.semaphore_signal(z_ready.at[outs[f[0]].index(f), l], inc=1, device_id=(f[0], c, h), device_id_type=MESH)
 
     @pl.when(l == 0)
     def _():
+        for t in range(rows):
+            below = [f for f in slots[t] if f[2] is None and f[0] < t]
+            if below:
+                @pl.when(p == t)
+                def _():
+                    for f in below:
+                        for b in range(1 if held_back(f) else 2):
+                            pl.semaphore_signal(z_ready.at[outs[f[0]].index(f)], inc=2, device_id=(f[0], c, b), device_id_type=MESH)
+        for k in direct:
+            @pl.when(jnp.logical_not(is_above(c, k)))
+            def _():
+                for h in range(2):
+                    pl.semaphore_signal(x_ready.at[k - 1], inc=1, device_id=(p, flip(c, k), h), device_id_type=MESH)
         pl.semaphore_signal(x_ready.at[2], inc=1, device_id=(p, c, other), device_id_type=MESH)
 
     load.wait()
@@ -125,23 +134,30 @@
     def z_copy(f, h, i):
         source = praw.at[0, l, pl.ds(h * half + i * piece, piece)]
         return remote(source, far_raw.at[slots[f[1]].index(f), l, pl.ds(i * piece, piece)],
-                      zs_sem.at[outs[f[0]].index(f), h, i], zr_sem.at[slots[f[1]].index(f), l, i], (f[1], c, h))
-
-    def z_arrival(t, b, i):
-        at = far_raw.at[t, b, pl.ds(pl.multiple_of(i * piece, piece), piece)]
-        return remote(at, at, zs_sem.at[0, 0, 0], zr_sem.at[t, b, i], (p, c, other))
-
-    def held_back(f):
-        return rows == 4 and f == (1, 2, None)
+                      far_sent, zr_sem.at[slots[f[1]].index(f), i], (f[1], c, h))
+
+    def landed(ref, sem):
+        remote(ref, ref, far_sent, sem, (p, c, other)).wait_recv()
+
+    def left(ref, sem):
+        remote(ref, ref, sem, zr_sem.at[0, 0], (p, c, other)).wait_send()
+
+    def far_here(t, i):
+        landed(far_raw.at[t, :, pl.ds(i * piece, piece)], zr_sem.at[t, i])
 
     def send_row(f, ask=False):
+        if ask:
+            if held_back(f):
+                @pl.when(l == 0)
+                def _():
+                    pl.semaphore_wait(z_ready.at[outs[f[0]].index(f)], 2)
+            else:
+                pl.semaphore_wait(z_ready.at[outs[f[0]].index(f)], 2)
         for i in range(cuts // 2 if held_back(f) else cuts):
             for h in (1, 0):
-                if ask and i == 0:
-                    pl.semaphore_wait(z_ready.at[outs[f[0]].index(f), h], 1)
                 z_copy(f, h, i).start()
 
-    exchange = remote(praw.at[0, l], praw.at[0, l], ex_sem.at[0], ex_sem.at[1], (p, c, other))
+    exchange = remote(praw.at[0, l], praw.at[0, l], own_sent, ex_sem, (p, c, other))
 
     @pl.when(l == 1)
     def _():
@@ -156,36 +172,50 @@
                 for f in down:
                     send_row(f)
 
-    def panel_copy(k, s):
-        at = pl.ds(s * half, half)
-        return remote(praw.at[0, l, at], praw.at[order.index(k), l, at], ps_sem.at[k - 1, s], pr_sem.at[k - 1, s],
+    def stage(k, s):
+        return {1: 1 - s, 2: s, 3: 2}.get(k, k - 1)
+
+    def stage_here(n, u):
+        landed(praw.at[0, l, pl.ds(0, half)], pr_sem.at[n, u])
+
+    def panel_copy(k, s, u):
+        at = pl.ds(s * half + u * half // 2, half // 2)
+        return remote(praw.at[0, l, at], praw.at[order.index(k), l, at], own_sent, pr_sem.at[stage(k, s), u],
                       (p, flip(c, k), l))
 
-    def pass_on(s):
+    def pass_on(s, u):
         source, target = (2, 1) if s == 0 else (1, 2)
-        at = pl.ds(s * half, half)
-        return remote(praw.at[order.index(source), l, at], praw.at[last, l, at], ps_sem.at[2, s], pr_sem.at[2, s],
+        at = pl.ds(s * half + u * half // 2, half // 2)
+        return remote(praw.at[order.index(source), l, at], praw.at[last, l, at], passed_sent, pr_sem.at[2, u],
                       (p, flip(c, target), l))
 
-    panel_copies = {(k, s): panel_copy(k, s) for k in direct for s in range(2)}
-    panel_copies.update({(3, s): pass_on(s) for s in range(2)})
-
-    def forward(k, s):
-        at = praw.at[order.index(k), l, pl.ds(s * half, half)]
-        return remote(at, at, fs_sem.at[k - 1, s], fr_sem.at[k - 1, s], (p, c, other))
+    panel_copies = {(k, s, u): panel_copy(k, s, u) for k in direct for s in range(2) for u in range(2)}
+    panel_copies.update({(3, s, u): pass_on(s, u) for s in range(2) for u in range(2)})
+
+    def forward(k, s, u):
+        at = praw.at[order.index(k), l, pl.ds(s * half + u * half // 2, half // 2)]
+        return remote(at, at, passed_sent, fr_sem.at[stage(k, s)], (p, c, other))
+
+    def complete(n):
+        landed(praw.at[0, other], fr_sem.at[n])
+        for k, s in places:
+            if k and stage(k, s) == n:
+                standardize(k, s)
 
     first = {1: (1, 0), 2: (0, 1)}
     for k in direct:
         @pl.when(jnp.logical_not(is_above(c, k)))
         def _():
             for s in first.get(k, (0, 1)):
-                panel_copies[k, s].start()
+                for u in range(2):
+                    panel_copies[k, s, u].start()
     for k in direct:
         @pl.when(is_above(c, k))
         def _():
             pl.semaphore_wait(x_ready.at[k - 1], 1)
             for s in first.get(k, (0, 1)):
-                panel_copies[k, s].start()
+                for u in range(2):
+                    panel_copies[k, s, u].start()
     for q in range(rows):
         up = [f for f in outs[q] if f[1] > q]
         if up:
@@ -267,27 +297,26 @@
     def relay_copy(f, b, i):
         at, t = pl.ds(i * piece, piece), slots[f[1]].index(f)
         return remote(far_raw.at[passed(f), b, at], far_raw.at[t, b, at],
-                      xs_sem.at[relays.index(f), b, i], zr_sem.at[t, b, i], (f[1], c, l))
+                      far_sent, zr_sem.at[t, i], (f[1], c, l))
 
     def relay(n, i):
         for f in relays[n:n + 1]:
             @pl.when(p == f[2])
             def _():
+                far_here(passed(f), i)
                 for b in range(2):
-                    z_arrival(passed(f), b, i).wait_recv()
                     relay_copy(f, b, i).start()
 
     for n, i in [(1, 0), (0, 0), (1, 1)]:
         relay(n, i)
-    for s in range(2):
-        panel_copies[2 - s, s].wait_recv()
-        panel_copies[3, s].start()
-        forward(2 - s, s).start()
+    for u in range(2):
+        stage_here(0, u)
+        for s in range(2):
+            panel_copies[3, s, u].start()
+            forward(2 - s, s, u).start()
     for n, i in [(0, 1), (1, 2)]:
         relay(n, i)
-    for s in range(2):
-        forward(2 - s, s).wait_recv()
-        standardize(2 - s, s)
+    complete(0)
     pairs(0, half, 2, 4)
     turn(2, 4)
     for n, i in [(1, 3), (0, 2)]:
@@ -299,9 +328,10 @@
                 for i in range(cuts // 2, cuts):
                     for h in (1, 0):
                         z_copy(f, h, i).start()
-    for s in range(2):
-        panel_copies[1 + s, s].wait_recv()
-        forward(1 + s, s).start()
+    for u in range(2):
+        stage_here(1, u)
+        for s in range(2):
+            forward(1 + s, s, u).start()
     relay(0, 3)
 
     def take_far(t, i):
@@ -309,15 +339,13 @@
         if passing:
             @pl.when(p != passing[0])
             def _():
-                for b in range(2):
-                    z_arrival(t, b, i).wait_recv()
+                far_here(t, i)
         else:
-            for b in range(2):
-                z_arrival(t, b, i).wait_recv()
+            far_here(t, i)
 
     def back_copy(f):
         t, j = slots[f[1]].index(f), back[f[0]].index(f)
-        return remote(rsrc.at[t], rdst.at[j], ts_sem.at[t], tr_sem.at[j], (f[0], c, l))
+        return remote(rsrc.at[t], rdst.at[j], back_sent, back_here, (f[0], c, l))
 
     def give_back(t):
         turned = racc[t * half:(t + 1) * half, :].T
@@ -348,20 +376,18 @@
             take_block(t)
             pairs(slot_at(t), slot_at(t) + half, 0, 4, True)
 
-    for s in range(2):
-        forward(1 + s, s).wait_recv()
-        standardize(1 + s, s)
+    complete(1)
     for k in direct[2:]:
+        for u in range(2):
+            stage_here(stage(k, 0), u)
+            for s in range(2):
+                forward(k, s, u).start()
+        complete(stage(k, 0))
+    pairs(0, middle, 4, ends - 2)
+    for u in range(2):
+        stage_here(2, u)
         for s in range(2):
-            panel_copies[k, s].wait_recv()
-            forward(k, s).start()
-        for s in range(2):
-            forward(k, s).wait_recv()
-            standardize(k, s)
-    pairs(0, middle, 4, ends - 2)
-    for s in range(2):
-        panel_copies[3, s].wait_recv()
-        forward(3, s).start()
+            forward(3, s, u).start()
     turn(4, ends - 2)
     for t in range(1, depth):
         @pl.when(n_slots > t)
@@ -375,37 +401,49 @@
                 take_block(t)
                 pairs(slot_at(t), slot_at(t) + half, 0, ends - 2, True)
 
-    for s in range(2):
-        forward(3, s).wait_recv()
-        standardize(3, s)
-    for t in range(1, depth):
-        @pl.when(n_slots > t)
-        def _():
-            pairs(slot_at(t), slot_at(t) + half, ends - 2, ends)
-            give_back(t)
-
-    pairs(0, middle, ends - 2, ends)
-    turn(ends - 2, ends)
-    for i in range(cuts // 2, cuts):
-        take_far(0, i)
-    standardize_far(0, half // 2, half)
-
     def part_copy(k, h):
-        return remote(psrc.at[k, h], pdst.at[k, l], qs_sem.at[k, h], qr_sem.at[k, l], (p, flip(c, k), h))
-
-    def part_arrival(k, b):
-        return remote(psrc.at[k, b], pdst.at[k, b], qs_sem.at[k, b], qr_sem.at[k, b], (p, c, other))
+        return remote(psrc.at[2 * k + h], pdst.at[2 * k + l], parts_sent, parts_here, (p, flip(c, k), h))
+
+    def take_last():
+        for i in range(cuts // 2, cuts):
+            take_far(0, i)
+        standardize_far(0, half // 2, half)
+
+    def finish_panel():
+        complete(2)
+        for t in range(1, depth):
+            @pl.when(n_slots > t)
+            def _():
+                pairs(slot_at(t), slot_at(t) + half, ends - 2, ends)
+                give_back(t)
 
     def send_parts(k):
         for h in range(2):
             place = places.index((k, h))
-            psrc[k, h] = pacc[:, place * half:(place + 1) * half]
+            psrc[2 * k + h] = pacc[:, place * half:(place + 1) * half]
             if k:
                 part_copy(k, h).start()
 
-    pairs(middle, 2 * half, ends - 2, ends, True)
-    send_parts(3)
-    pairs(middle, 2 * half, 0, ends - 2, True)
+    waits = by_row([1 if any(held_back(f) or f[2] is not None for f in slots[q]) else 0 for q in range(rows)]) == 1
+
+    @pl.when(waits)
+    def _():
+        finish_panel()
+        pairs(0, middle, ends - 2, ends)
+        turn(ends - 2, ends)
+        take_last()
+        pairs(middle, 2 * half, ends - 2, ends, True)
+        send_parts(3)
+        pairs(middle, 2 * half, 0, ends - 2, True)
+
+    @pl.when(jnp.logical_not(waits))
+    def _():
+        take_last()
+        pairs(middle, 2 * half, 0, ends - 2, True)
+        finish_panel()
+        pairs(0, 2 * half, ends - 2, ends)
+        send_parts(3)
+
     sums_first = p < rows // 2
 
     @pl.when(jnp.logical_not(sums_first))
@@ -420,52 +458,34 @@
     def _():
         give_back(0)
 
-    exchange.wait_send()
-    for k, s in panel_copies:
-        panel_copies[k, s].wait_send()
-        forward(k, s).wait_send()
-    for k in range(1, cols):
-        for h in range(2):
-            part_copy(k, h).wait_send()
-    part_copy(0, other).wait_send()
+    left(praw.at[pl.ds(0, last), l], own_sent)
+    left(praw.at[:, l], passed_sent)
+    left(psrc.at[pl.ds(0, 2 * cols - 1)], parts_sent)
     for q in range(rows):
         @pl.when(p == q)
         def _():
-            for f in outs[q]:
-                for h in range(2):
-                    for i in range(cuts):
-                        z_copy(f, h, i).wait_send()
-            for f in relays:
-                if f[2] == q:
-                    for b in range(2):
-                        for i in range(cuts):
-                            relay_copy(f, b, i).wait_send()
-            for f in slots[q]:
-                back_copy(f).wait_send()
-
-    total = psrc[0, l] - 1.0 / 8
-    part_arrival(0, other).wait_recv()
-    total = total + pdst[0, other]
-    for k in range(1, cols):
-        for b in range(2):
-            part_arrival(k, b).wait_recv()
-            total = total + pdst[k, b]
-
-    def back_arrival(j):
-        return remote(rsrc.at[0], rdst.at[j], ts_sem.at[0], tr_sem.at[j], (p, c, other))
-
-    n_back = by_row([len(back[q]) for q in range(rows)])
-    least = min(len(back[q]) for q in range(rows))
-    for j in range(least):
-        back_arrival(j).wait_recv()
-        total = total + rdst[j]
-    psrc[0, l] = total
-    for j in range(least, max(len(back[q]) for q in range(rows))):
-        @pl.when(n_back > j)
-        def _():
-            back_arrival(j).wait_recv()
-            psrc[0, l] += rdst[j]
-    out_ref[...] = jnp.sum(psrc[0, l], axis=0)
+            blocks = len(outs[q]) + len([f for f in relays if f[2] == q])
+            if blocks:
+                left(praw.at[pl.ds(0, blocks), l], far_sent)
+            if slots[q]:
+                left(rsrc.at[pl.ds(0, len(slots[q]))], back_sent)
+
+    total = psrc[l] - 1.0 / 8
+    landed(pdst.at[pl.ds(0, 2 * cols - 1)], parts_here)
+    total = total + pdst[other]
+    for n in range(2, 2 * cols):
+        total = total + pdst[n]
+    psrc[l] = total
+    for q in range(rows):
+        if back[q]:
+            @pl.when(p == q)
+            def _():
+                landed(rdst.at[pl.ds(0, len(back[q]))], back_here)
+                more = rdst[0]
+                for j in range(1, len(back[q])):
+                    more = more + rdst[j]
+                psrc[l] += more
+    out_ref[...] = jnp.sum(psrc[l], axis=0)
 
 
 def solution(mesh):
@@ -492,20 +512,15 @@
                 pltpu.VMEM(((1 + depth) * half, samples), bf16),
                 pltpu.VMEM((8, cols * genes), f32),
                 pltpu.VMEM((depth * half, 128), f32),
-                pltpu.VMEM((cols, 2, 8, half), f32),
-                pltpu.VMEM((cols, 2, 8, half), f32),
+                pltpu.VMEM((2 * cols, 8, half), f32),
+                pltpu.VMEM((2 * cols, 8, half), f32),
                 pltpu.VMEM((depth, 8, half), f32),
                 pltpu.VMEM((fan, 8, half), f32),
-                pltpu.SemaphoreType.DMA,
-                dma(2),
-                dma(cols - 1, 2), dma(cols - 1, 2),
-                dma(cols - 1, 2), dma(cols - 1, 2),
-                dma(fan, 2, 4), dma(depth, 2, 4),
-                dma(max(len([f for f in flows if f[2] is not None]), 1), 2, 4),
-                dma(cols, 2), dma(cols, 2),
-                dma(depth), dma(fan),
+                *[pltpu.SemaphoreType.DMA] * 7,
+                dma(cols - 1, 2), dma(cols - 1), dma(depth, 4),
+                pltpu.SemaphoreType.DMA, pltpu.SemaphoreType.DMA,
                 pltpu.SemaphoreType.REGULAR((cols - 1,)),
-                pltpu.SemaphoreType.REGULAR((fan, 2)),
+                pltpu.SemaphoreType.REGULAR((fan,)),
             ],
             compiler_params=pltpu.CompilerParams(collective_id=0, has_side_effects=True, vmem_limit_bytes=48000000),
         )(pltpu.with_memory_space_constraint(expression, pltpu.HBM))

time: 26.4 us -> 25.9 us (0.981)
  Pallas kernels: 25.7 us -> 25.2 us
    pallas_call x1, Pallas kernels: 25.7 us -> 25.2 us  [on_device(): pl.pallas_call(functools.partial(kernel, rows, cols), out_shape=jax.Shape...]
where the time goes in v7:
time: 25.9 us; the launch traced here: 25.8 us
  Pallas kernels  25.2 us (97%)
  local copies, waits for them, and re-layouts  0.56 us (2%)
    pallas_call x1, Pallas kernels, on_device(): pl.pallas_call(functools.partial(kernel, rows, cols), out_shape=jax.Shape...  25.2 us
    unnamed x1, local copies, waits for them, and re-layouts  0.56 us

profile of v7, /device:TPU:17, one launch (start us, length us, event | category | flops | bytes accessed | tf_op | source)
XLA Modules:
  0.0 25.8 jit_solution(9536262785636939450)
XLA Ops:
  0.0 25.2 %shard_map.17 = f32[192]{0:T(256)S(1)} custom-call(bf16[384,512]{1,0:T(8,128)(2,1)} %x_ref.1), custom_call_target="tpu_custom_call" | custom-call | tf_op jit(solution)/shard_map/pallas_call | solution.py:502
  25.2 0.6 %copy.3 = f32[192]{0:T(256)} copy(f32[192]{0:T(256)S(1)} %shard_map.17) | data formatting | bytes 1536

commit v8 on v7

--- a/solution.py
+++ b/solution.py
@@ -102,12 +102,14 @@
                         greet((t, c, h))
                 for f in slots[q]:
                     if held_back(f):
-                        greet((f[0], c, 1))
+                        @pl.when(l == 1)
+                        def _():
+                            greet((f[0], c, 1))
     greetings = jnp.where(alone, 1, other) + by_row([2 * len([t for t in pairs_of[q] if t < q]) for q in range(rows)])
     for k in direct:
         greetings = greetings + jnp.where(is_above(c, k), 0, 2)
 
-    greetings = greetings + l * by_row([2 * len([f for f in outs[q] if held_back(f)]) for q in range(rows)])
+    greetings = greetings + l * by_row([len([f for f in outs[q] if held_back(f)]) for q in range(rows)])
     pacc[...] = jnp.zeros_like(pacc)
     racc[...] = jnp.zeros_like(racc)
     pl.semaphore_wait(barrier, greetings)
@@ -120,7 +122,7 @@
                 @pl.when(p == t)
                 def _():
                     for f in below:
-                        for b in range(1 if held_back(f) else 2):
+                        for b in range(2):
                             pl.semaphore_signal(z_ready.at[outs[f[0]].index(f)], inc=2, device_id=(f[0], c, b), device_id_type=MESH)
         for k in direct:
             @pl.when(jnp.logical_not(is_above(c, k)))
@@ -146,16 +148,21 @@
         landed(far_raw.at[t, :, pl.ds(i * piece, piece)], zr_sem.at[t, i])
 
     def send_row(f, ask=False):
-        if ask:
-            if held_back(f):
-                @pl.when(l == 0)
+        ready = z_ready.at[outs[f[0]].index(f)]
+        if held_back(f):
+            for h in (1, 0):
+                @pl.when(l == 1 - h)
                 def _():
-                    pl.semaphore_wait(z_ready.at[outs[f[0]].index(f)], 2)
-            else:
-                pl.semaphore_wait(z_ready.at[outs[f[0]].index(f)], 2)
-        for i in range(cuts // 2 if held_back(f) else cuts):
-            for h in (1, 0):
-                z_copy(f, h, i).start()
+                    pl.semaphore_wait(ready, 2)
+
+                for i in range(cuts // 2):
+                    z_copy(f, h, i).start()
+        else:
+            if ask:
+                pl.semaphore_wait(ready, 2)
+            for i in range(cuts):
+                for h in (1, 0):
+                    z_copy(f, h, i).start()
 
     exchange = remote(praw.at[0, l], praw.at[0, l], own_sent, ex_sem, (p, c, other))
 
@@ -248,10 +255,10 @@
         return (1 + t) * half
 
     def standardize_far(t, first, stop):
-        for j in range(first // step, stop // step):
-            at = pl.ds(j * step, step)
+        for j in range(first // piece, stop // piece):
+            at = pl.ds(j * piece, piece)
             low, high = scale(far_raw[t, 0, at, :], far_raw[t, 1, at, :])
-            at = pl.ds(slot_at(t) + j * step, step)
+            at = pl.ds(slot_at(t) + j * piece, piece)
             stack[at, 0:part] = low
             stack[at, part:samples] = high
 
@@ -326,7 +333,7 @@
             @pl.when(p == f[0])
             def _():
                 for i in range(cuts // 2, cuts):
-                    for h in (1, 0):
+                    for h in ((1, 0) if i < cuts - 1 else (0, 1)):
                         z_copy(f, h, i).start()
     for u in range(2):
         stage_here(1, u)
@@ -424,19 +431,34 @@
             if k:
                 part_copy(k, h).start()
 
-    waits = by_row([1 if any(held_back(f) or f[2] is not None for f in slots[q]) else 0 for q in range(rows)]) == 1
-
-    @pl.when(waits)
+    kind = by_row([2 if any(held_back(f) for f in slots[q]) else 1 if slots[q] and slots[q][0][2] is not None else 0
+                   for q in range(rows)])
+
+    @pl.when(kind == 2)
     def _():
         finish_panel()
         pairs(0, middle, ends - 2, ends)
         turn(ends - 2, ends)
+        final = 2 * half - piece
+        for i in range(cuts // 2, cuts - 1):
+            take_far(0, i)
+        standardize_far(0, half // 2, half - piece)
+        pairs(middle, final, 0, ends, True)
+        take_far(0, cuts - 1)
+        standardize_far(0, half - piece, half)
+        pairs(final, 2 * half, ends - 2, ends, True)
+        send_parts(3)
+        pairs(final, 2 * half, 0, ends - 2, True)
+
+    @pl.when(kind == 1)
+    def _():
+        finish_panel()
         take_last()
-        pairs(middle, 2 * half, ends - 2, ends, True)
+        pairs(0, 2 * half, ends - 2, ends)
         send_parts(3)
         pairs(middle, 2 * half, 0, ends - 2, True)
 
-    @pl.when(jnp.logical_not(waits))
+    @pl.when(kind == 0)
     def _():
         take_last()
         pairs(middle, 2 * half, 0, ends - 2, True)
@@ -446,12 +468,14 @@
 
     sums_first = p < rows // 2
 
+    for k in direct:
+        send_parts(k)
+
     @pl.when(jnp.logical_not(sums_first))
     def _():
         give_back(0)
 
-    for k in direct + [0]:
-        send_parts(k)
+    send_parts(0)
     part_copy(0, other).start()
 
     @pl.when(sums_first)

time: 25.9 us -> 25.4 us (0.981)
  the two profiles are of different devices: /device:TPU:17 before, /device:TPU:0 now
where the time goes in v8:
time: 25.4 us; the launch traced here: 25.3 us
  Pallas kernels  24.7 us (97%)
  local copies, waits for them, and re-layouts  0.56 us (2%)
    pallas_call x1, Pallas kernels, on_device(): pl.pallas_call(functools.partial(kernel, rows, cols), out_shape=jax.Shape...  24.7 us
    unnamed x1, local copies, waits for them, and re-layouts  0.56 us

profile of v8, /device:TPU:0, one launch (start us, length us, event | category | flops | bytes accessed | tf_op | source)
XLA Modules:
  0.0 25.3 jit_solution(3719886610964968106)
XLA Ops:
  0.0 24.7 %shard_map.17 = f32[192]{0:T(256)S(1)} custom-call(bf16[384,512]{1,0:T(8,128)(2,1)} %x_ref.1), custom_call_target="tpu_custom_call" | custom-call | tf_op jit(solution)/shard_map/pallas_call | solution.py:526
  24.7 0.6 %copy.3 = f32[192]{0:T(256)} copy(f32[192]{0:T(256)S(1)} %shard_map.17) | data formatting | bytes 1536

commit v9 on v8

--- a/solution.py
+++ b/solution.py
@@ -59,6 +59,9 @@
     def held_back(f):
         return rows == 4 and f == (1, 2, None)
 
+    def quick(f):
+        return rows == 4 and f in ((0, 1, None), (1, 2, None))
+
     def remote(src, dst, send, recv, device):
         return pltpu.make_async_remote_copy(
             src_ref=src, dst_ref=dst, send_sem=send, recv_sem=recv, device_id=device, device_id_type=MESH
@@ -94,14 +97,14 @@
                 greet((p, flip(c, k), h))
     for q in range(rows):
         above = [t for t in pairs_of[q] if t > q]
-        if above or any(held_back(f) for f in slots[q]):
+        if above or any(quick(f) for f in slots[q]):
             @pl.when(p == q)
             def _():
                 for t in above:
                     for h in range(2):
                         greet((t, c, h))
                 for f in slots[q]:
-                    if held_back(f):
+                    if quick(f):
                         @pl.when(l == 1)
                         def _():
                             greet((f[0], c, 1))
@@ -109,7 +112,7 @@
     for k in direct:
         greetings = greetings + jnp.where(is_above(c, k), 0, 2)
 
-    greetings = greetings + l * by_row([len([f for f in outs[q] if held_back(f)]) for q in range(rows)])
+    greetings = greetings + l * by_row([len([f for f in outs[q] if quick(f)]) for q in range(rows)])
     pacc[...] = jnp.zeros_like(pacc)
     racc[...] = jnp.zeros_like(racc)
     pl.semaphore_wait(barrier, greetings)
@@ -150,19 +153,17 @@
     def send_row(f, ask=False):
         ready = z_ready.at[outs[f[0]].index(f)]
         if held_back(f):
-            for h in (1, 0):
-                @pl.when(l == 1 - h)
+            order_of = [(h, i) for h in (1, 0) for i in range(cuts // 2)]
+        else:
+            order_of = [(h, i) for i in range(cuts) for h in (1, 0)]
+        early = order_of.index((0, 0)) if quick(f) else 0
+        for n, (h, i) in enumerate(order_of):
+            if ask and n in (0, early):
+                @pl.when(jnp.logical_or(early == 0, l == (1 if n else 0)))
                 def _():
                     pl.semaphore_wait(ready, 2)
 
-                for i in range(cuts // 2):
-                    z_copy(f, h, i).start()
-        else:
-            if ask:
-                pl.semaphore_wait(ready, 2)
-            for i in range(cuts):
-                for h in (1, 0):
-                    z_copy(f, h, i).start()
+            z_copy(f, h, i).start()
 
     exchange = remote(praw.at[0, l], praw.at[0, l], own_sent, ex_sem, (p, c, other))
 
@@ -325,9 +326,8 @@
         relay(n, i)
     complete(0)
     pairs(0, half, 2, 4)
-    turn(2, 4)
-    for n, i in [(1, 3), (0, 2)]:
-        relay(n, i)
+    relay(0, 2)
+    relay(1, 3)
     for f in flows:
         if held_back(f):
             @pl.when(p == f[0])
@@ -335,6 +335,7 @@
                 for i in range(cuts // 2, cuts):
                     for h in ((1, 0) if i < cuts - 1 else (0, 1)):
                         z_copy(f, h, i).start()
+    turn(2, 4)
     for u in range(2):
         stage_here(1, u)
         for s in range(2):
@@ -544,7 +545,7 @@
                 dma(cols - 1, 2), dma(cols - 1), dma(depth, 4),
                 pltpu.SemaphoreType.DMA, pltpu.SemaphoreType.DMA,
                 pltpu.SemaphoreType.REGULAR((cols - 1,)),
-                pltpu.SemaphoreType.REGULAR((fan,)),
+                pltpu.SemaphoreType.REGULAR((max(len([f for f in flows if f[0] == q and f[2] is None]) for q in range(rows)),)),
             ],
             compiler_params=pltpu.CompilerParams(collective_id=0, has_side_effects=True, vmem_limit_bytes=48000000),
         )(pltpu.with_memory_space_constraint(expression, pltpu.HBM))

time: 25.4 us -> 25.4 us (level); the launches traced: 25.3 us -> 25 us
  Pallas kernels: 24.7 us -> 24.4 us
    pallas_call x1, Pallas kernels: 24.7 us -> 24.4 us  [on_device(): pl.pallas_call(functools.partial(kernel, rows, cols), out_shape=jax.Shape...]
where the time goes in v9:
time: 25.4 us; the launch traced here: 25 us
  Pallas kernels  24.4 us (96%)
  local copies, waits for them, and re-layouts  0.56 us (2%)
    pallas_call x1, Pallas kernels, on_device(): pl.pallas_call(functools.partial(kernel, rows, cols), out_shape=jax.Shape...  24.4 us
    unnamed x1, local copies, waits for them, and re-layouts  0.56 us

profile of v9, /device:TPU:0, one launch (start us, length us, event | category | flops | bytes accessed | tf_op | source)
XLA Modules:
  0.0 25.0 jit_solution(5030691133687143293)
XLA Ops:
  0.0 24.4 %shard_map.17 = f32[192]{0:T(256)S(1)} custom-call(bf16[384,512]{1,0:T(8,128)(2,1)} %x_ref.1), custom_call_target="tpu_custom_call" | custom-call | tf_op jit(solution)/shard_map/pallas_call | solution.py:527
  24.4 0.6 %copy.3 = f32[192]{0:T(256)} copy(f32[192]{0:T(256)S(1)} %shard_map.17) | data formatting | bytes 1536

commit v10 on v9

--- a/solution.py
+++ b/solution.py
@@ -36,8 +36,8 @@
 
 
 def kernel(rows, cols, x_ref, out_ref, praw, panel, across, far_raw, stack, pacc, racc, psrc, pdst, rsrc, rdst,
-           in_sem, ex_sem, own_sent, passed_sent, far_sent, parts_sent, back_sent,
-           pr_sem, fr_sem, zr_sem, parts_here, back_here, x_ready, z_ready):
+           ex_sem, own_sent, far_sent, parts_sent,
+           pr_sem, fr_sem, zr_sem, parts_here, x_ready, z_ready):
     p, c, l = lax.axis_index("row"), lax.axis_index("col"), lax.axis_index("layer")
     genes, part = x_ref.shape
     half = genes // 2
@@ -76,7 +76,7 @@
     def at_row(q, condition=True):
         return pl.when(p == q)
 
-    load = pltpu.make_async_copy(x_ref, praw.at[0, l], in_sem)
+    load = pltpu.make_async_copy(x_ref, praw.at[0, l], parts_sent)
     load.start()
 
     barrier = pltpu.get_barrier_semaphore()
@@ -194,7 +194,7 @@
     def pass_on(s, u):
         source, target = (2, 1) if s == 0 else (1, 2)
         at = pl.ds(s * half + u * half // 2, half // 2)
-        return remote(praw.at[order.index(source), l, at], praw.at[last, l, at], passed_sent, pr_sem.at[2, u],
+        return remote(praw.at[order.index(source), l, at], praw.at[last, l, at], own_sent, pr_sem.at[2, u],
                       (p, flip(c, target), l))
 
     panel_copies = {(k, s, u): panel_copy(k, s, u) for k in direct for s in range(2) for u in range(2)}
@@ -202,7 +202,7 @@
 
     def forward(k, s, u):
         at = praw.at[order.index(k), l, pl.ds(s * half + u * half // 2, half // 2)]
-        return remote(at, at, passed_sent, fr_sem.at[stage(k, s)], (p, c, other))
+        return remote(at, at, own_sent, fr_sem.at[stage(k, s)], (p, c, other))
 
     def complete(n):
         landed(praw.at[0, other], fr_sem.at[n])
@@ -353,7 +353,7 @@
 
     def back_copy(f):
         t, j = slots[f[1]].index(f), back[f[0]].index(f)
-        return remote(rsrc.at[t], rdst.at[j], back_sent, back_here, (f[0], c, l))
+        return remote(rsrc.at[t], rdst.at[j], parts_sent, parts_here, (f[0], c, l))
 
     def give_back(t):
         turned = racc[t * half:(t + 1) * half, :].T
@@ -426,7 +426,7 @@
                 give_back(t)
 
     def send_parts(k):
-        for h in range(2):
+        for h in (1, 0):
             place = places.index((k, h))
             psrc[2 * k + h] = pacc[:, place * half:(place + 1) * half]
             if k:
@@ -483,34 +483,27 @@
     def _():
         give_back(0)
 
-    left(praw.at[pl.ds(0, last), l], own_sent)
-    left(praw.at[:, l], passed_sent)
-    left(psrc.at[pl.ds(0, 2 * cols - 1)], parts_sent)
+    left(panel.at[pl.ds(0, (2 * cols - 1) * half)], own_sent)
     for q in range(rows):
         @pl.when(p == q)
         def _():
             blocks = len(outs[q]) + len([f for f in relays if f[2] == q])
             if blocks:
                 left(praw.at[pl.ds(0, blocks), l], far_sent)
-            if slots[q]:
-                left(rsrc.at[pl.ds(0, len(slots[q]))], back_sent)
-
-    total = psrc[l] - 1.0 / 8
-    landed(pdst.at[pl.ds(0, 2 * cols - 1)], parts_here)
-    total = total + pdst[other]
+            left(psrc.at[pl.ds(0, 2 * cols - 1 + len(slots[q]))], parts_sent)
+
+    for q in range(rows):
+        @pl.when(p == q)
+        def _():
+            landed(pdst.at[pl.ds(0, 2 * cols - 1 + len(back[q]))], parts_here)
+            more = psrc[l] - 1.0 / 8
+            for j in range(len(back[q])):
+                more = more + rdst[j]
+            psrc[l] = more
+    total = psrc[l] + pdst[other]
     for n in range(2, 2 * cols):
         total = total + pdst[n]
-    psrc[l] = total
-    for q in range(rows):
-        if back[q]:
-            @pl.when(p == q)
-            def _():
-                landed(rdst.at[pl.ds(0, len(back[q]))], back_here)
-                more = rdst[0]
-                for j in range(1, len(back[q])):
-                    more = more + rdst[j]
-                psrc[l] += more
-    out_ref[...] = jnp.sum(psrc[l], axis=0)
+    out_ref[...] = jnp.sum(total, axis=0)
 
 
 def solution(mesh):
@@ -537,13 +530,13 @@
                 pltpu.VMEM(((1 + depth) * half, samples), bf16),
                 pltpu.VMEM((8, cols * genes), f32),
                 pltpu.VMEM((depth * half, 128), f32),
-                pltpu.VMEM((2 * cols, 8, half), f32),
-                pltpu.VMEM((2 * cols, 8, half), f32),
+                pltpu.VMEM((2 * cols + depth, 8, half), f32),
+                pltpu.VMEM((2 * cols + fan, 8, half), f32),
                 pltpu.VMEM((depth, 8, half), f32),
                 pltpu.VMEM((fan, 8, half), f32),
-                *[pltpu.SemaphoreType.DMA] * 7,
+                *[pltpu.SemaphoreType.DMA] * 4,
                 dma(cols - 1, 2), dma(cols - 1), dma(depth, 4),
-                pltpu.SemaphoreType.DMA, pltpu.SemaphoreType.DMA,
+                pltpu.SemaphoreType.DMA,
                 pltpu.SemaphoreType.REGULAR((cols - 1,)),
                 pltpu.SemaphoreType.REGULAR((max(len([f for f in flows if f[0] == q and f[2] is None]) for q in range(rows)),)),
             ],

time: 25.4 us -> 25.2 us (level)
  no operation moved by 1% of the time
where the time goes in v10:
time: 25.2 us; the launch traced here: 24.9 us
  Pallas kernels  24.4 us (97%)
  local copies, waits for them, and re-layouts  0.56 us (2%)
    pallas_call x1, Pallas kernels, on_device(): pl.pallas_call(functools.partial(kernel, rows, cols), out_shape=jax.Shape...  24.4 us
    unnamed x1, local copies, waits for them, and re-layouts  0.56 us

profile of v10, /device:TPU:0, one launch (start us, length us, event | category | flops | bytes accessed | tf_op | source)
XLA Modules:
  0.0 24.9 jit_solution(15018794426645176310)
XLA Ops:
  0.0 24.4 %shard_map.17 = f32[192]{0:T(256)S(1)} custom-call(bf16[384,512]{1,0:T(8,128)(2,1)} %x_ref.1), custom_call_target="tpu_custom_call" | custom-call | tf_op jit(solution)/shard_map/pallas_call | solution.py:520
  24.4 0.6 %copy.3 = f32[192]{0:T(256)} copy(f32[192]{0:T(256)S(1)} %shard_map.17) | data formatting | bytes 1536

commit v11 on v10

--- a/solution.py
+++ b/solution.py
@@ -184,17 +184,20 @@
         return {1: 1 - s, 2: s, 3: 2}.get(k, k - 1)
 
     def stage_here(n, u):
-        landed(praw.at[0, l, pl.ds(0, half)], pr_sem.at[n, u])
+        if n:
+            landed(praw.at[0, l, pl.ds(0, half)], pr_sem.at[2 * n + u - 1])
+        elif u == 0:
+            landed(praw.at[0, l], pr_sem.at[0])
 
     def panel_copy(k, s, u):
         at = pl.ds(s * half + u * half // 2, half // 2)
-        return remote(praw.at[0, l, at], praw.at[order.index(k), l, at], own_sent, pr_sem.at[stage(k, s), u],
+        return remote(praw.at[0, l, at], praw.at[order.index(k), l, at], own_sent, pr_sem.at[max(2 * stage(k, s) + u - 1, 0)],
                       (p, flip(c, k), l))
 
     def pass_on(s, u):
         source, target = (2, 1) if s == 0 else (1, 2)
         at = pl.ds(s * half + u * half // 2, half // 2)
-        return remote(praw.at[order.index(source), l, at], praw.at[last, l, at], own_sent, pr_sem.at[2, u],
+        return remote(praw.at[order.index(source), l, at], praw.at[last, l, at], own_sent, pr_sem.at[3 + u],
                       (p, flip(c, target), l))
 
     panel_copies = {(k, s, u): panel_copy(k, s, u) for k in direct for s in range(2) for u in range(2)}
@@ -535,7 +538,7 @@
                 pltpu.VMEM((depth, 8, half), f32),
                 pltpu.VMEM((fan, 8, half), f32),
                 *[pltpu.SemaphoreType.DMA] * 4,
-                dma(cols - 1, 2), dma(cols - 1), dma(depth, 4),
+                dma(2 * cols - 3), dma(cols - 1), dma(depth, 4),
                 pltpu.SemaphoreType.DMA,
                 pltpu.SemaphoreType.REGULAR((cols - 1,)),
                 pltpu.SemaphoreType.REGULAR((max(len([f for f in flows if f[0] == q and f[2] is None]) for q in range(rows)),)),

time: 25.2 us -> 25.2 us (level)
  no operation moved by 1% of the time
where the time goes in v11:
time: 25.2 us; the launch traced here: 24.9 us
  Pallas kernels  24.4 us (97%)
  local copies, waits for them, and re-layouts  0.56 us (2%)
    pallas_call x1, Pallas kernels, on_device(): pl.pallas_call(functools.partial(kernel, rows, cols), out_shape=jax.Shape...  24.4 us
    unnamed x1, local copies, waits for them, and re-layouts  0.56 us

profile of v11, /device:TPU:0, one launch (start us, length us, event | category | flops | bytes accessed | tf_op | source)
XLA Modules:
  0.0 24.9 jit_solution(17427554797761954343)
XLA Ops:
  0.0 24.4 %shard_map.17 = f32[192]{0:T(256)S(1)} custom-call(bf16[384,512]{1,0:T(8,128)(2,1)} %x_ref.1), custom_call_target="tpu_custom_call" | custom-call | tf_op jit(solution)/shard_map/pallas_call | solution.py:523
  24.4 0.6 %copy.3 = f32[192]{0:T(256)} copy(f32[192]{0:T(256)S(1)} %shard_map.17) | data formatting | bytes 1536
